TPU v7x, 256 devices: a whole 4x4x8 slice. The times are simulated.
256 devices in a mesh: arcs: 2 (over z_lo), trow: 8 (over y, core), tcol: 16 (over x, z_hi).
Axes of the slice: x: 4, y: 4, z: 8 (z_hi: 4, z_lo: 2; z = z_hi * 2 + z_lo), core: 2. Of those that a mesh axis runs over, the one named last changes fastest.
Arguments:
- design: bfloat16 [4096, 12288], P(('arcs', 'tcol'), 'trow'), may hold values from -6 to 6
- observed: float32 [4096], P(('arcs', 'tcol')), may hold values from -6 to 6
- arc_counts: int32 [128], P(('arcs', 'tcol')), may hold values from 2 to 32
- arc_weight: float32 [128], P(('arcs', 'tcol')), may hold values from 0.3 to 3
Outputs:
- gram: float32 [12288, 12288], P('trow', ('arcs', 'tcol'))
- rhs: float32 [12288], P('trow')
Inputs may be any that keep to these rules, and one draw needn't show every extreme that they name: `arc_counts`: each arc has at least two valid observations.
All inputs are finite; a program needn't handle non-finite values.
Results may differ from a plain program's by a relative error of at most 0.0055.
Values may be sent and summed in bfloat16 or wider, within the bound.
No kernel may reach another device: no remote copies, remote signals or barrier semaphores. Data moves between devices by JAX's collectives and lax.ppermute only.
A program may use at most 192 MiB of HBM per device.

v0:
```python
import jax
import jax.numpy as jnp
from jax import lax
from jax.sharding import PartitionSpec as P


def from_everyone(x, axis):
    devices = lax.axis_size(axis)
    return lax.all_to_all(jnp.broadcast_to(x[None], (devices, *x.shape)), axis, 0, 0, tiled=True)


def over_copies(x, axis):
    return from_everyone(x, axis).sum(axis=0)


def cut_along(x, dim, devices):
    dims = x.shape
    blocks = x.reshape(*dims[:dim], devices, dims[dim] // devices, *dims[dim + 1 :])
    return jnp.moveaxis(blocks, dim, 0)


def sum_at_owner(x, axis, dim):
    blocks = cut_along(x, dim, lax.axis_size(axis))
    arrived = lax.all_to_all(blocks, axis, split_axis=0, concat_axis=0, tiled=True)
    return arrived.astype(jnp.float32).sum(axis=0)


def fold_with(right, piece):
    return lax.dot_general(
        piece, right, (((0,), (0,)), ((), ())), preferred_element_type=jnp.float32
    )


def local(design, observed, arc_counts, arc_weight):
    row_count, col_width = design.shape
    arc_total = arc_counts.shape[0]
    arc_len = row_count // arc_total
    slot_index = lax.broadcasted_iota(jnp.int32, (arc_total, arc_len), 1)
    valid_mask = (slot_index < arc_counts[:, None]).astype(jnp.float32)
    counts_float = arc_counts.astype(jnp.float32)
    factor = valid_mask * jnp.sqrt(arc_weight)[:, None]
    blocks = design.reshape(arc_total, arc_len, col_width).astype(jnp.float32)
    column_mean = jnp.sum(valid_mask[:, :, None] * blocks, axis=1) / counts_float[:, None]
    centered = (
        (factor[:, :, None] * (blocks - column_mean[:, None, :]))
        .reshape(row_count, col_width)
        .astype(jnp.bfloat16)
    )
    series = observed.reshape(arc_total, arc_len)
    series_mean = jnp.sum(valid_mask * series, axis=1) / counts_float
    weighted = (factor * (series - series_mean[:, None])).reshape(row_count)
    arc_devices = lax.axis_size("arcs")
    tcol_devices = lax.axis_size("tcol")
    obs_total = row_count * arc_devices * tcol_devices
    rhs_part = jnp.dot(weighted, centered.astype(jnp.float32), precision=lax.Precision.HIGHEST)
    rhs = over_copies(rhs_part, ("arcs", "tcol")) * obs_total ** (-0.5)
    every_coef = lax.all_gather(centered, "trow", axis=1, tiled=True)
    full_width = every_coef.shape[1]
    narrow = full_width // (arc_devices * tcol_devices)
    shaped = every_coef.reshape(row_count, arc_devices, tcol_devices, narrow)
    moved = lax.all_to_all(shaped, "tcol", split_axis=2, concat_axis=0, tiled=True)
    right = moved.reshape(row_count * tcol_devices, arc_devices * narrow)
    partial_value = fold_with(right, lax.all_gather(centered, "tcol", axis=0, tiled=True))
    tile = sum_at_owner(partial_value.astype(jnp.bfloat16), "arcs", 1)
    gram = tile * (1.0 / obs_total)
    return (gram, rhs)


def solution(mesh):
    return jax.shard_map(
        local,
        mesh=mesh,
        in_specs=(
            P(("arcs", "tcol"), "trow"),
            P(("arcs", "tcol")),
            P(("arcs", "tcol")),
            P(("arcs", "tcol")),
        ),
        out_specs=(P("trow", ("arcs", "tcol")), P("trow")),
        check_vma=False,
    )
```

profile of v0, /device:TPU:1, one launch (start us, length us, event | category | flops | bytes accessed | tf_op | source)
XLA Modules:
  0.0 264.2 jit_solution(5195800618479505239)
XLA Ops:
  7.2 0.0 all-gather.5.cloned.1.call-start
  7.2 0.7 fusion.4
  7.9 0.7 convert_element_type.33
  8.6 0.7 reshape.101
  9.3 0.7 sqrt.3
  10.0 1.4 select_reduce_fusion
  11.3 0.1 mul.48
  11.4 1.2 multiply_reduce_fusion
  12.6 0.1 broadcast_divide_fusion
  12.7 1.9 fusion.3
  14.6 0.0 all-gather.5.cloned.1.call-update
  14.6 0.0 all-gather.3.cloned.1.call-start
  14.6 0.7 all-gather.3.cloned.1.call-update
  15.3 33.9 %all-gather.5.cloned.1.call-done = bf16[128,12288]{1,0:T(8,128)(2,1)} async-done(((bf16[128,1536]{1,0:T(8,128)(2,1)}), bf16[128,12288]{1,0:T(8,128)(2,1)}) %all-gather.5.cloned.1.call-update) | async-done | bytes 3145744 | tf_op jit(solution)/shard_map/all_gather | solution.py:57
  49.2 3.5 %copy.21 = bf16[128,12288]{0,1:T(8,128)(2,1)S(1)} copy(bf16[128,12288]{1,0:T(8,128)(2,1)} %all-gather.5.cloned.1.call-done) | data formatting | bytes 6291456 | tf_op jit(solution)/shard_map/all_gather | solution.py:57
  52.7 1.9 copy.22
  54.6 0.0 copy-start.2
  54.6 0.0 copy-start
  54.6 0.0 copy-start.1
  54.6 9.4 %all-to-all-start = ((bf16[128,2,16,384]{0,3,1,2:T(8,128)(2,1)}), bf16[128,2,16,384]{0,3,1,2:T(8,128)(2,1)S(1)}, u32[]{:S(2)}, u32[]{:S(2)}) async-start(bf16[128,2,16,384]{0,3,1,2:T(8,128)(2,1)} %copy.22), calls=%async_computation | async-start | bytes 6291456 | tf_op jit(solution)/shard_map/all_to_all | solution.py:61
  64.0 0.0 copy-done.2
  64.0 0.7 convert_divide_fusion
  64.7 0.1 sub.25
  64.7 0.6 sub.26
  65.3 0.0 copy-done
  65.3 0.0 copy-done.1
  65.3 0.9 convolution_reduce_fusion
  66.3 82.1 %all-to-all-done = bf16[128,2,16,384]{0,3,1,2:T(8,128)(2,1)S(1)} async-done(((bf16[128,2,16,384]{0,3,1,2:T(8,128)(2,1)}), bf16[128,2,16,384]{0,3,1,2:T(8,128)(2,1)S(1)}, u32[]{:S(2)}, u32[]{:S(2)}) %all-to-all-start) | async-done | bytes 3145760 | tf_op jit(solution)/shard_map/all_to_all | solution.py:61
  148.4 0.8 broadcast_in_dim.2
  149.2 10.1 %all-to-all-start.2 = ((f32[32,1,1536]{2,1,0:T(1,128)}), f32[32,1,1536]{2,1,0:T(1,128)S(1)}, u32[]{:S(2)}, u32[]{:S(2)}) async-start(f32[32,1,1536]{2,1,0:T(1,128)} %broadcast_in_dim.2), calls=%async_computation.2 | async-start | bytes 393216 | tf_op jit(solution)/shard_map/all_to_all | solution.py:9
  159.2 3.7 %copy.23 = bf16[16,128,2,1,384]{1,0,4,2,3:T(8,128)(2,1)} copy(bf16[16,128,2,1,384]{1,4,2,0,3:T(8,128)(2,1)S(1)} %bitcast.27) | data formatting | bytes 6291456 | tf_op jit(solution)/shard_map/all_to_all | solution.py:61
  163.0 51.0 %all-gather.3.cloned.1.call-done = bf16[2048,1536]{1,0:T(8,128)(2,1)} async-done(((bf16[128,1536]{1,0:T(8,128)(2,1)}), bf16[2048,1536]{1,0:T(8,128)(2,1)}) %all-gather.3.cloned.1.call-update) | async-done | bytes 6291472 | tf_op jit(solution)/shard_map/all_gather | solution.py:63
  213.9 9.5 %convolution_convert_fusion = bf16[1536,768]{0,1:T(8,128)(2,1)} fusion(bf16[2048,1536]{1,0:T(8,128)(2,1)} %all-gather.3.cloned.1.call-done, bf16[96,8,16,128]{3,2,1,0:T(8,128)(2,1)} %bitcast.29), kind=kOutput, calls=%fused_computation.1 | convolution fusion | flops 4833017856 | bytes 11796480 | tf_op jit(solution)/shard_map/dot_general | solution.py:29
  223.4 0.0 all-to-all-done.2
  223.4 3.8 %all-to-all-start.1 = ((bf16[2,1536,384]{1,2,0:T(8,128)(2,1)}), bf16[2,1536,384]{1,2,0:T(8,128)(2,1)S(1)}, u32[]{:S(2)}, u32[]{:S(2)}) async-start(bf16[2,1536,384]{1,2,0:T(8,128)(2,1)} %bitcast.30), calls=%async_computation.1 | async-start | bytes 4718592 | tf_op jit(solution)/shard_map/all_to_all | solution.py:24
  227.3 0.1 reduce_sum.39
  227.4 0.6 broadcast_multiply_fusion.1
  228.0 26.8 %all-to-all-done.1 = bf16[2,1536,384]{1,2,0:T(8,128)(2,1)S(1)} async-done(((bf16[2,1536,384]{1,2,0:T(8,128)(2,1)}), bf16[2,1536,384]{1,2,0:T(8,128)(2,1)S(1)}, u32[]{:S(2)}, u32[]{:S(2)}) %all-to-all-start.1) | async-done | bytes 2359328 | tf_op jit(solution)/shard_map/all_to_all | solution.py:24
  254.8 0.4 convert_reduce_fusion
  255.2 0.2 broadcast_multiply_fusion
  255.4 2.0 copy.25
Async XLA Ops:
  7.2 42.0 %all-gather.5.cloned.1.call-start = ((), (), s32[]{:S(2)}) async-start(), calls=%async_computation.4 | async-start | bytes 3538944 | tf_op jit(solution)/shard_map/all_gather | solution.py:57
  14.6 199.3 %all-gather.3.cloned.1.call-start = ((), (), s32[]{:S(2)}) async-start(), calls=%async_computation.3 | async-start | bytes 6684672 | tf_op jit(solution)/shard_map/all_gather | solution.py:63
  54.6 9.4 %copy-start.2 = (s32[4]{0:T(128)S(1)}, s32[4]{0:T(128)}, u32[]{:S(2)}) copy-start(s32[4]{0:T(128)} %param.6) | copy-start | bytes 52
  54.6 10.7 %copy-start = (bf16[128,1536]{1,0:T(8,128)(2,1)S(1)}, bf16[128,1536]{1,0:T(8,128)(2,1)}, u32[]{:S(2)}) copy-start(bf16[128,1536]{1,0:T(8,128)(2,1)} %fusion.3) | copy-start | bytes 1179652
  54.6 10.7 %copy-start.1 = (f32[128]{0:T(128)S(1)}, f32[128]{0:T(128)}, u32[]{:S(2)}) copy-start(f32[128]{0:T(128)} %param.5) | copy-start | bytes 1540
  54.6 93.8 %all-to-all-start = ((bf16[128,2,16,384]{0,3,1,2:T(8,128)(2,1)}), bf16[128,2,16,384]{0,3,1,2:T(8,128)(2,1)S(1)}, u32[]{:S(2)}, u32[]{:S(2)}) async-start(bf16[128,2,16,384]{0,3,1,2:T(8,128)(2,1)} %copy.22), calls=%async_computation | async-start | bytes 6291456 | tf_op jit(solution)/shard_map/all_to_all | solution.py:61
  149.2 74.3 %all-to-all-start.2 = ((f32[32,1,1536]{2,1,0:T(1,128)}), f32[32,1,1536]{2,1,0:T(1,128)S(1)}, u32[]{:S(2)}, u32[]{:S(2)}) async-start(f32[32,1,1536]{2,1,0:T(1,128)} %broadcast_in_dim.2), calls=%async_computation.2 | async-start | bytes 393216 | tf_op jit(solution)/shard_map/all_to_all | solution.py:9
  223.4 31.3 %all-to-all-start.1 = ((bf16[2,1536,384]{1,2,0:T(8,128)(2,1)}), bf16[2,1536,384]{1,2,0:T(8,128)(2,1)S(1)}, u32[]{:S(2)}, u32[]{:S(2)}) async-start(bf16[2,1536,384]{1,2,0:T(8,128)(2,1)} %bitcast.30), calls=%async_computation.1 | async-start | bytes 4718592 | tf_op jit(solution)/shard_map/all_to_all | solution.py:24
Sparse Core Ops, SparseCore 0:
  14.7 34.4 all-gather.4
  52.2 161.6 all-gather.2
where the time goes:
time: 265 us; the launch traced here: 264 us
  waiting for transfers between devices  194 us (73%)
  starting transfers between devices  23.3 us (9%)
  between operations  14.1 us (5%)
  local copies, waits for them, and re-layouts  14 us (5%)
  matrix products  10.4 us (4%)
  other arithmetic  7.85 us (3%)
    all_to_all x1, waiting for transfers between devices, local(): lax.all_to_all(shaped, 'tcol', split_axis=2, concat_axis=0, tiled=True)  82.1 us
    all_gather x1, waiting for transfers between devices, local(): lax.all_gather(centered, 'tcol', axis=0, tiled=True)  51 us
    all_gather x1, waiting for transfers between devices, local(): every_coef = lax.all_gather(centered, 'trow', axis=1, tiled=True)  33.9 us
    all_to_all x1, waiting for transfers between devices, sum_at_owner(): lax.all_to_all(blocks, axis, split_axis=0, concat_axis=0, tiled=True)  26.8 us
    all_to_all x1, starting transfers between devices, from_everyone(): lax.all_to_all(jnp.broadcast_to(x[None], (devices, *x.shape)), axis, 0, 0...  10.1 us
    dot_general x1, matrix products, fold_with(): lax.dot_general(piece, right, (((0,), (0,)), ((), ())), preferred_element...  9.51 us
    all_to_all x1, starting transfers between devices, local(): lax.all_to_all(shaped, 'tcol', split_axis=2, concat_axis=0, tiled=True)  9.38 us
  transfers between devices with their start and end apart: 5, of which 4 were waited for; matrix products, arithmetic and copies ran while one was open for 8% of the time, Pallas kernels for 0%

commit v1 on v0

v1 whole, which is shorter than its diff:
```python
import jax
import jax.numpy as jnp
from jax import lax
from jax.experimental import pallas as pl
from jax.experimental.pallas import tpu as pltpu
from jax.sharding import PartitionSpec as P


AXES = ("arcs", "trow", "tcol")


def device_index(x, y, core, zh, zl):
    return (zl * 8 + y * 2 + core) * 16 + x * 4 + zh


def moved(value, where):
    pairs = []
    for x in range(4):
        for y in range(4):
            for core in range(2):
                for zh in range(4):
                    for zl in range(2):
                        pairs.append(
                            (device_index(x, y, core, zh, zl), device_index(*where(x, y, core, zh, zl)))
                        )
    return lax.ppermute(value, AXES, pairs)


def along_z(step):
    def where(x, y, core, zh, zl):
        z = (zh * 2 + zl + step) % 8
        return x, y, core, z // 2, z % 2

    return where


def round_y(x, y, core, zh, zl):
    return x, (y + (1 if core == 0 else 3)) % 4, core, zh, zl


def other_core(x, y, core, zh, zl):
    return x, y, 1 - core, zh, zl


def first_x(x, y, core, zh, zl):
    return x ^ (1 if core == 0 else 3), y, core, zh, zl


def second_x(x, y, core, zh, zl):
    return x ^ (3 if core == 0 else 1), y, core, zh, zl


def flip_z(mask):
    def where(x, y, core, zh, zl):
        z = (zh * 2 + zl) ^ mask
        return x, y, core, z // 2, z % 2

    return where


def to_share(turn):
    def where(x, y, core, zh, zl):
        a = y // 2
        return x, (y if zl == a else 3 - y), core, (zh + turn) % 4, a

    return where


def centre(where_ref, *refs):
    sources, out_ref, share_refs, rhs_ref = refs[:4], refs[4], refs[5:9], refs[9]
    counts_ref, weight_ref, design_ref, observed_ref = refs[10:14]
    copies = [pltpu.make_async_copy(sources[i], refs[10 + i], refs[14].at[i]) for i in range(4)]
    for copy in copies:
        copy.start()
    for copy in copies:
        copy.wait()
    arcs = counts_ref.shape[0]
    rows, cols = design_ref.shape
    length = rows // arcs
    slot = lax.broadcasted_iota(jnp.int32, (length, 1), 0)
    lane = lax.broadcasted_iota(jnp.int32, (1, rows), 1)
    observed = observed_ref[...]
    weighted = jnp.zeros((1, rows), jnp.float32)
    for arc in range(arcs):
        count = counts_ref[arc]
        mask = (slot < count).astype(jnp.float32)
        total = jnp.full((1, 1), count.astype(jnp.float32))
        root = jnp.sqrt(jnp.full((1, 1), weight_ref[arc]))
        piece = design_ref[pl.ds(arc * length, length), :].astype(jnp.float32)
        mean = jnp.sum(mask * piece, axis=0, keepdims=True) / total
        out_ref[pl.ds(arc * length, length), :] = ((mask * root) * (piece - mean)).astype(jnp.bfloat16)
        inside = ((lane >= arc * length) & (lane < arc * length + count)).astype(jnp.float32)
        series_mean = jnp.sum(inside * observed, axis=1, keepdims=True) / total
        weighted = weighted + (inside * root) * (observed - series_mean)
    high = weighted.astype(jnp.bfloat16)
    rest1 = weighted - high.astype(jnp.float32)
    middle = rest1.astype(jnp.bfloat16)
    low = (rest1 - middle.astype(jnp.float32)).astype(jnp.bfloat16)
    row = lax.broadcasted_iota(jnp.int32, (8, rows), 0)
    parts = jnp.where(
        row == 0,
        high.astype(jnp.float32),
        jnp.where(row == 1, middle.astype(jnp.float32), jnp.where(row == 2, low.astype(jnp.float32), 0.0)),
    ).astype(jnp.bfloat16)
    sums = jnp.dot(parts, out_ref[...], preferred_element_type=jnp.float32)
    rhs_ref[...] = jnp.sum(sums, axis=0, keepdims=True)
    narrow = cols // 4
    for turn, share_ref in enumerate(share_refs):
        start = pl.multiple_of(((where_ref[3] + turn) % 4) * narrow, 128)
        share_ref[...] = out_ref[:, pl.ds(start, narrow)]


def place(where_ref, *refs):
    rows_refs, column_refs, rows_out, cols_out = refs[:9], refs[9:-2], refs[-2], refs[-1]
    x, y, core, zh, zl = (where_ref[i] for i in range(5))
    start = 0
    for ref in rows_refs:
        rows_out[pl.ds(start, ref.shape[0]), :] = ref[...]
        start += ref.shape[0]
    z = 2 * zh + zl
    behind = jnp.where(core == 0, 3, 1)
    first = jnp.where(core == 0, 1, 3)

    def put(source_core, offset, ref):
        from_y = (y + offset) % 4
        near = from_y // 2 == zl
        of_y = jnp.where(near, from_y, 3 - from_y)
        of_zl = jnp.where(near, zl, 1 - zl)
        m = (2 * (of_y % 2) + source_core) ^ x
        spot = jnp.where(m == 0, 0, jnp.where(m == 2, 3, jnp.where(m == first, 2, 1)))
        for turn in range(4):
            of_z = 2 * ((zh + 4 - turn) % 4) + of_zl
            ahead = (of_z + 8 - z) % 8
            cols_out[
                spot // 2,
                pl.ds(pl.multiple_of(ahead * 128, 128), 128),
                pl.ds(pl.multiple_of((spot % 2) * 384, 128), 384),
            ] = ref[turn]

    share, c0, y1, y1c, c1, c1c, y2, c2 = column_refs
    put(core, 0, share)
    put(1 - core, 0, c0)
    put(core, behind, y1)
    put(1 - core, behind, y1c)
    put(1 - core, 4 - behind, c1)
    put(core, 4 - behind, c1c)
    put(core, 2, y2)
    put(1 - core, 2, c2)


def product(left, right):
    return lax.dot_general(left, right, (((0,), (0,)), ((), ())), preferred_element_type=jnp.float32)


VMEM = pl.BlockSpec(memory_space=pltpu.VMEM)
SMEM = pl.BlockSpec(memory_space=pltpu.SMEM)


def local(design, observed, arc_counts, arc_weight):
    rows, cols = design.shape
    narrow = cols // 4
    obs_total = 4096
    bf16, f32 = jnp.bfloat16, jnp.float32
    trow, tcol = lax.axis_index("trow"), lax.axis_index("tcol")
    where = jnp.stack([tcol // 4, trow // 2, trow % 2, tcol % 4, lax.axis_index("arcs")])

    out = pl.pallas_call(
        centre,
        out_shape=[jax.ShapeDtypeStruct((rows, cols), bf16)]
        + [jax.ShapeDtypeStruct((rows, narrow), bf16)] * 4
        + [jax.ShapeDtypeStruct((1, cols), f32)],
        in_specs=[SMEM] + [pl.BlockSpec(memory_space=pltpu.HBM)] * 4,
        out_specs=[VMEM] * 6,
        scratch_shapes=[
            pltpu.SMEM(arc_counts.shape, arc_counts.dtype),
            pltpu.SMEM(arc_weight.shape, arc_weight.dtype),
            pltpu.VMEM(design.shape, design.dtype),
            pltpu.VMEM((1, rows), f32),
            pltpu.SemaphoreType.DMA((4,)),
        ],
        compiler_params=pltpu.CompilerParams(vmem_limit_bytes=8 << 20),
        name="centre",
    )(where, arc_counts, arc_weight, design, observed.reshape(1, rows))
    centered, shares, rhs = out[0], out[1:5], out[5].reshape(cols)

    up, down = [centered], [centered]
    for _ in range(1, 4):
        up.append(moved(up[-1], along_z(1)))
        down.append(moved(down[-1], along_z(-1)))
    far_up = moved(up[3][: rows // 2], along_z(1))
    far_down = moved(down[3][rows // 2 :], along_z(-1))
    pieces = [centered, *down[1:], far_up, far_down, up[3], up[2], up[1]]

    share = jnp.concatenate([moved(shares[turn], to_share(turn))[None] for turn in range(4)])
    c0 = moved(share, other_core)
    y1, y1c = moved(share, round_y), moved(c0, round_y)
    c1, c1c = moved(y1, other_core), moved(y1c, other_core)
    y2 = moved(y1, round_y)
    columns = [share, c0, y1, y1c, c1, c1c, y2, moved(y2, other_core)]

    every_row, right = pl.pallas_call(
        place,
        out_shape=[
            jax.ShapeDtypeStruct((8 * rows, cols), bf16),
            jax.ShapeDtypeStruct((2, 8 * rows, 2 * narrow), bf16),
        ],
        in_specs=[SMEM] + [VMEM] * 17,
        out_specs=[VMEM] * 2,
        compiler_params=pltpu.CompilerParams(vmem_limit_bytes=20 << 20),
        name="place",
    )(where, *pieces, *columns)

    send = product(every_row, right[1]).astype(bf16)
    got = moved(send, first_x).astype(f32)
    keep = lax.optimization_barrier(product(every_row, right[0]))
    last = moved((keep[:, narrow:] + got[:, narrow:]).astype(bf16), second_x)
    gram = (keep[:, :narrow] + got[:, :narrow] + last.astype(f32)) * (1.0 / obs_total)

    for mask in (1, 2, 4):
        rhs = rhs + moved(rhs, flip_z(mask))
    rhs = rhs + moved(rhs, second_x)
    rhs = rhs + moved(rhs, first_x)
    return (gram, rhs * obs_total ** (-0.5))


def solution(mesh):
    return jax.shard_map(
        local,
        mesh=mesh,
        in_specs=(
            P(("arcs", "tcol"), "trow"),
            P(("arcs", "tcol")),
            P(("arcs", "tcol")),
            P(("arcs", "tcol")),
        ),
        out_specs=(P("trow", ("arcs", "tcol")), P("trow")),
        check_vma=False,
    )
```

time: 265 us -> 134 us (0.51)
  the two profiles are of different devices: /device:TPU:1 before, /device:TPU:16 now
where the time goes in v1:
time: 134 us
  waiting for transfers between devices  69.8 us (52%)
  starting transfers between devices  44.5 us (33%)
  other arithmetic  5.61 us (4%)
  matrix products  5.61 us (4%)
  local copies, waits for them, and re-layouts  4.85 us (4%)
  Pallas kernels  2.76 us (2%)
    ppermute x26, waiting for transfers between devices, moved(): return lax.ppermute(value, AXES, pairs)  69.8 us
    ppermute x26, starting transfers between devices, moved(): return lax.ppermute(value, AXES, pairs)  44.5 us
    dot_general x2, matrix products, product(): lax.dot_general(left, right, (((0,), (0,)), ((), ())), preferred_element_...  5.61 us
    unnamed x12, local copies, waits for them, and re-layouts  4.74 us
    mul x1, other arithmetic, local(): (keep[:, :narrow] + got[:, :narrow] + last.astype(f32)) * (1.0 / obs_total)  4.19 us
  transfers between devices with their start and end apart: 26, of which 15 were waited for; matrix products, arithmetic and copies ran while one was open for 3% of the time, Pallas kernels for 0%

profile of v1, /device:TPU:16, one launch (start us, length us, event | category | flops | bytes accessed | tf_op | source)
XLA Modules:
  0.0 133.9 jit_solution(6400157826100938839)
XLA Ops:
  0.7 0.1 stack.23.where_ref
  0.8 1.0 copy-done
  1.8 0.7 copy-done.1
  2.4 0.7 copy-done.2
  3.1 0.7 copy-done.3
  3.7 1.6 %centre.1 = (bf16[128,1536]{1,0:T(8,128)(2,1)S(1)}, bf16[128,384]{1,0:T(8,128)(2,1)S(1)}, bf16[128,384]{1,0:T(8,128)(2,1)S(1)}, bf16[128,384]{1,0:T(8,128)(2,1)S...) custom-call(s32[5]{0:T(128)S(1)} %stack.23.where_ref, s32[4]{0:T(128)S(1)} %copy-done.1, f32[4]{0:T(128)S(1)} %copy-done.2, ...), custom_call_target="tpu_custom_call" | custom-call | tf_op jit(solution)/shard_map/centre/pallas_call | solution.py:167
  5.3 3.7 %collective-permute-start.8 = (bf16[128,384]{1,0:T(8,128)(2,1)S(1)}, bf16[128,384]{1,0:T(8,128)(2,1)S(1)}, u32[]{:S(2)}, u32[]{:S(2)}) collective-permute-start(bf16[128,384]{1,0:T(8,128)(2,1)S(1)} %get-tuple-element.11), channel_id=1, source_target_pairs={{0,0},{128,96},{1,1},{129,97},{2,2},{130,98},{3,3},{131,99},{16,16... | collective-permute-start | bytes 294920 | tf_op jit(solution)/shard_map/ppermute | solution.py:26
  9.0 3.9 %collective-permute-start.9 = (bf16[128,384]{1,0:T(8,128)(2,1)S(1)}, bf16[128,384]{1,0:T(8,128)(2,1)S(1)}, u32[]{:S(2)}, u32[]{:S(2)}) collective-permute-start(bf16[128,384]{1,0:T(8,128)(2,1)S(1)} %get-tuple-element.12), channel_id=1, source_target_pairs={{0,1},{128,97},{1,2},{129,98},{2,3},{130,99},{3,0},{131,96},{16,17... | collective-permute-start | bytes 294920 | tf_op jit(solution)/shard_map/ppermute | solution.py:26
  12.9 3.9 %collective-permute-start.10 = (bf16[128,384]{1,0:T(8,128)(2,1)S(1)}, bf16[128,384]{1,0:T(8,128)(2,1)S(1)}, u32[]{:S(2)}, u32[]{:S(2)}) collective-permute-start(bf16[128,384]{1,0:T(8,128)(2,1)S(1)} %get-tuple-element.13), channel_id=1, source_target_pairs={{0,2},{128,98},{1,3},{129,99},{2,0},{130,96},{3,1},{131,97},{16,18... | collective-permute-start | bytes 294920 | tf_op jit(solution)/shard_map/ppermute | solution.py:26
  16.9 4.1 %collective-permute-start.11 = (bf16[128,384]{1,0:T(8,128)(2,1)S(1)}, bf16[128,384]{1,0:T(8,128)(2,1)S(1)}, u32[]{:S(2)}, u32[]{:S(2)}) collective-permute-start(bf16[128,384]{1,0:T(8,128)(2,1)S(1)} %get-tuple-element.14), channel_id=1, source_target_pairs={{0,3},{128,99},{1,0},{129,96},{2,1},{130,97},{3,2},{131,98},{16,19... | collective-permute-start | bytes 294920 | tf_op jit(solution)/shard_map/ppermute | solution.py:26
  21.0 0.0 collective-permute-start.3
  21.0 0.0 collective-permute-done.8
  21.0 3.2 %collective-permute-start = (bf16[128,1536]{1,0:T(8,128)(2,1)S(1)}, bf16[128,1536]{1,0:T(8,128)(2,1)S(1)}, u32[]{:S(2)}, u32[]{:S(2)}) collective-permute-start(bf16[128,1536]{1,0:T(8,128)(2,1)S(1)} %get-tuple-element.10.refs_0_), channel_id=1, source_target_pairs={{0,131},{128,0},{1,128},{129,1},{2,129},{130,2},{3,130},{131,3},{1... | collective-permute-start | bytes 1179656 | tf_op jit(solution)/shard_map/ppermute | solution.py:26
  24.2 0.0 collective-permute-done.9
  24.2 1.9 %collective-permute-done.10 = bf16[128,384]{1,0:T(8,128)(2,1)S(1)} collective-permute-done((bf16[128,384]{1,0:T(8,128)(2,1)S(1)}, bf16[128,384]{1,0:T(8,128)(2,1)S(1)}, u32[]{:S(2)}, u32[]{:S(2)}) %collective-permute-start.10) | collective-permute-done | bytes 98336 | tf_op jit(solution)/shard_map/ppermute | solution.py:26
  26.2 1.2 collective-permute-done.11
  27.4 0.1 pad_maximum_fusion.refs_9_
  27.5 0.1 collective-permute-start.12
  27.6 3.0 %collective-permute-start.13 = (bf16[4,128,384]{2,1,0:T(8,128)(2,1)S(1)}, bf16[4,128,384]{2,1,0:T(8,128)(2,1)S(1)}, u32[]{:S(2)}, u32[]{:S(2)}) collective-permute-start(bf16[4,128,384]{2,1,0:T(8,128)(2,1)S(1)} %pad_maximum_fusion.refs_9_), channel_id=1, source_target_pairs={{0,32},{128,160},{1,33},{129,161},{2,34},{130,162},{3,35},{131,163... | collective-permute-start | bytes 1179656 | tf_op jit(solution)/shard_map/ppermute | solution.py:26
  30.6 1.3 %collective-permute-done.3.refs_8_ = bf16[128,1536]{1,0:T(8,128)(2,1)S(1)} collective-permute-done((bf16[128,1536]{1,0:T(8,128)(2,1)S(1)}, bf16[128,1536]{1,0:T(8,128)(2,1)S(1)}, u32[]{:S(2)}, u32[]{:S(2)}) %collective-permute-start.3) | collective-permute-done | bytes 393248 | tf_op jit(solution)/shard_map/ppermute | solution.py:26
  31.9 0.0 collective-permute-start.4
  32.0 3.8 %collective-permute-done.refs_1_ = bf16[128,1536]{1,0:T(8,128)(2,1)S(1)} collective-permute-done((bf16[128,1536]{1,0:T(8,128)(2,1)S(1)}, bf16[128,1536]{1,0:T(8,128)(2,1)S(1)}, u32[]{:S(2)}, u32[]{:S(2)}) %collective-permute-start) | collective-permute-done | bytes 393248 | tf_op jit(solution)/shard_map/ppermute | solution.py:26
  35.7 3.7 %collective-permute-start.1 = (bf16[128,1536]{1,0:T(8,128)(2,1)S(1)}, bf16[128,1536]{1,0:T(8,128)(2,1)S(1)}, u32[]{:S(2)}, u32[]{:S(2)}) collective-permute-start(bf16[128,1536]{1,0:T(8,128)(2,1)S(1)} %collective-permute-done.refs_1_), channel_id=1, source_target_pairs={{0,131},{128,0},{1,128},{129,1},{2,129},{130,2},{3,130},{131,3},{1... | collective-permute-start | bytes 1179656 | tf_op jit(solution)/shard_map/ppermute | solution.py:26
  39.4 0.0 collective-permute-done.12.refs_10_
  39.4 1.3 collective-permute-start.14
  40.7 0.0 collective-permute-done.13.refs_11_
  40.7 0.1 collective-permute-start.17
  40.8 1.4 %collective-permute-done.4.refs_7_ = bf16[128,1536]{1,0:T(8,128)(2,1)S(1)} collective-permute-done((bf16[128,1536]{1,0:T(8,128)(2,1)S(1)}, bf16[128,1536]{1,0:T(8,128)(2,1)S(1)}, u32[]{:S(2)}, u32[]{:S(2)}) %collective-permute-start.4) | collective-permute-done | bytes 393248 | tf_op jit(solution)/shard_map/ppermute | solution.py:26
  42.2 0.0 collective-permute-start.5
  42.2 5.8 %collective-permute-done.1.refs_2_ = bf16[128,1536]{1,0:T(8,128)(2,1)S(1)} collective-permute-done((bf16[128,1536]{1,0:T(8,128)(2,1)S(1)}, bf16[128,1536]{1,0:T(8,128)(2,1)S(1)}, u32[]{:S(2)}, u32[]{:S(2)}) %collective-permute-start.1) | collective-permute-done | bytes 393248 | tf_op jit(solution)/shard_map/ppermute | solution.py:26
  48.0 3.7 %collective-permute-start.2 = (bf16[128,1536]{1,0:T(8,128)(2,1)S(1)}, bf16[128,1536]{1,0:T(8,128)(2,1)S(1)}, u32[]{:S(2)}, u32[]{:S(2)}) collective-permute-start(bf16[128,1536]{1,0:T(8,128)(2,1)S(1)} %collective-permute-done.1.refs_2_), channel_id=1, source_target_pairs={{0,131},{128,0},{1,128},{129,1},{2,129},{130,2},{3,130},{131,3},{1... | collective-permute-start | bytes 1179656 | tf_op jit(solution)/shard_map/ppermute | solution.py:26
  51.7 0.0 collective-permute-start.15
  51.7 0.0 collective-permute-done.14.refs_12_
  51.7 0.5 collective-permute-start.16
  52.2 0.1 collective-permute-start.18
  52.3 0.8 collective-permute-done.5.refs_6_
  53.1 0.3 collective-permute-start.6
  53.3 6.0 %collective-permute-done.2.refs_3_ = bf16[128,1536]{1,0:T(8,128)(2,1)S(1)} collective-permute-done((bf16[128,1536]{1,0:T(8,128)(2,1)S(1)}, bf16[128,1536]{1,0:T(8,128)(2,1)S(1)}, u32[]{:S(2)}, u32[]{:S(2)}) %collective-permute-start.2) | collective-permute-done | bytes 393248 | tf_op jit(solution)/shard_map/ppermute | solution.py:26
  59.4 3.8 %collective-permute-start.7 = (bf16[64,1536]{1,0:T(8,128)(2,1)S(1)}, bf16[64,1536]{1,0:T(8,128)(2,1)S(1)}, u32[]{:S(2)}, u32[]{:S(2)}) collective-permute-start(bf16[64,1536]{1,0:T(8,128)(2,1)S(1)} %slice.33), channel_id=1, source_target_pairs={{0,131},{128,0},{1,128},{129,1},{2,129},{130,2},{3,130},{131,3},{1... | collective-permute-start | bytes 589832 | tf_op jit(solution)/shard_map/ppermute | solution.py:26
  63.2 0.0 collective-permute-done.15.refs_13_
  63.2 0.0 collective-permute-done.16.refs_14_
  63.2 0.0 collective-permute-done.6.refs_4_
  63.2 3.2 %collective-permute-done.7.refs_5_ = bf16[64,1536]{1,0:T(8,128)(2,1)S(1)} collective-permute-done((bf16[64,1536]{1,0:T(8,128)(2,1)S(1)}, bf16[64,1536]{1,0:T(8,128)(2,1)S(1)}, u32[]{:S(2)}, u32[]{:S(2)}) %collective-permute-start.7) | collective-permute-done | bytes 196640 | tf_op jit(solution)/shard_map/ppermute | solution.py:26
  66.4 1.2 place.1
  67.5 2.9 %convolution_convert_fusion = bf16[1536,768]{1,0:T(8,128)(2,1)S(1)} fusion(bf16[1024,1536]{1,0:T(8,128)(2,1)S(1)} %get-tuple-element.15, bf16[2,1024,768]{2,1,0:T(8,128)(2,1)S(1)} %get-tuple-element.16), kind=kOutput, calls=%fused_computation | convolution fusion | flops 2417098752 | bytes 7077888 | tf_op jit(solution)/shard_map/dot_general | solution.py:152
  70.5 1.6 %collective-permute-start.19 = (bf16[1536,768]{1,0:T(8,128)(2,1)S(1)}, bf16[1536,768]{1,0:T(8,128)(2,1)S(1)}, u32[]{:S(2)}, u32[]{:S(2)}) collective-permute-start(bf16[1536,768]{1,0:T(8,128)(2,1)S(1)} %convolution_convert_fusion), channel_id=1, source_target_pairs={{0,4},{128,132},{1,5},{129,133},{2,6},{130,134},{3,7},{131,135},{1... | collective-permute-start | bytes 7077896 | tf_op jit(solution)/shard_map/ppermute | solution.py:26
  72.0 2.7 %fusion.4 = f32[1536,768]{1,0:T(8,128)S(1)} fusion(bf16[1024,1536]{1,0:T(8,128)(2,1)S(1)} %get-tuple-element.15, bf16[2,1024,768]{2,1,0:T(8,128)(2,1)S(1)} %get-tuple-element.16), kind=kOutput, calls=%fused_computation.7 | convolution fusion | flops 2415919104 | bytes 9437184 | tf_op jit(solution)/shard_map/dot_general | solution.py:152
  74.7 24.7 %collective-permute-done.19 = bf16[1536,768]{1,0:T(8,128)(2,1)S(1)} collective-permute-done((bf16[1536,768]{1,0:T(8,128)(2,1)S(1)}, bf16[1536,768]{1,0:T(8,128)(2,1)S(1)}, u32[]{:S(2)}, u32[]{:S(2)}) %collective-permute-start.19) | collective-permute-done | bytes 2359328 | tf_op jit(solution)/shard_map/ppermute | solution.py:26
  99.4 0.4 convert_element_type.13
  99.8 0.4 fusion
  100.2 1.8 %copy-done.4 = f32[1536,768]{1,0:T(8,128)} copy-done((f32[1536,768]{1,0:T(8,128)}, f32[1536,768]{1,0:T(8,128)S(1)}, u32[]{:S(2)}) %copy-start.4) | copy-done | bytes 4718616
  101.9 2.8 %collective-permute-start.20 = (bf16[1536,384]{1,0:T(8,128)(2,1)S(1)}, bf16[1536,384]{1,0:T(8,128)(2,1)S(1)}, u32[]{:S(2)}, u32[]{:S(2)}) collective-permute-start(bf16[1536,384]{1,0:T(8,128)(2,1)S(1)} %fusion), channel_id=1, source_target_pairs={{0,12},{128,140},{1,13},{129,141},{2,14},{130,142},{3,15},{131,143... | collective-permute-start | bytes 3538952 | tf_op jit(solution)/shard_map/ppermute | solution.py:26
  104.7 0.1 collective-permute-start.21
  104.8 3.6 %collective-permute-done.21 = f32[1536]{0:T(1024)S(1)} collective-permute-done((f32[1536]{0:T(1024)S(1)}, f32[1536]{0:T(1024)S(1)}, u32[]{:S(2)}, u32[]{:S(2)}) %collective-permute-start.21) | collective-permute-done | bytes 6176 | tf_op jit(solution)/shard_map/ppermute | solution.py:26
  108.5 1.5 %collective-permute-start.22 = (f32[1536]{0:T(1024)S(1)}, f32[1536]{0:T(1024)S(1)}, u32[]{:S(2)}, u32[]{:S(2)}) collective-permute-start(f32[1536]{0:T(1024)S(1)} %add.38), channel_id=1, source_target_pairs={{0,1},{128,129},{1,0},{129,128},{2,3},{130,131},{3,2},{131,130},{1... | collective-permute-start | bytes 18440 | tf_op jit(solution)/shard_map/ppermute | solution.py:26
  110.0 3.0 %collective-permute-done.22 = f32[1536]{0:T(1024)S(1)} collective-permute-done((f32[1536]{0:T(1024)S(1)}, f32[1536]{0:T(1024)S(1)}, u32[]{:S(2)}, u32[]{:S(2)}) %collective-permute-start.22) | collective-permute-done | bytes 6176 | tf_op jit(solution)/shard_map/ppermute | solution.py:26
  113.0 2.6 %collective-permute-start.23 = (f32[1536]{0:T(1024)S(1)}, f32[1536]{0:T(1024)S(1)}, u32[]{:S(2)}, u32[]{:S(2)}) collective-permute-start(f32[1536]{0:T(1024)S(1)} %add.39), channel_id=1, source_target_pairs={{0,2},{128,130},{1,3},{129,131},{2,0},{130,128},{3,1},{131,129},{1... | collective-permute-start | bytes 18440 | tf_op jit(solution)/shard_map/ppermute | solution.py:26
  115.6 5.0 %collective-permute-done.23 = f32[1536]{0:T(1024)S(1)} collective-permute-done((f32[1536]{0:T(1024)S(1)}, f32[1536]{0:T(1024)S(1)}, u32[]{:S(2)}, u32[]{:S(2)}) %collective-permute-start.23) | collective-permute-done | bytes 6176 | tf_op jit(solution)/shard_map/ppermute | solution.py:26
  120.6 0.5 collective-permute-start.24
  121.0 4.4 %collective-permute-done.24 = f32[1536]{0:T(1024)S(1)} collective-permute-done((f32[1536]{0:T(1024)S(1)}, f32[1536]{0:T(1024)S(1)}, u32[]{:S(2)}, u32[]{:S(2)}) %collective-permute-start.24) | collective-permute-done | bytes 6176 | tf_op jit(solution)/shard_map/ppermute | solution.py:26
  125.5 3.6 %collective-permute-done.25 = f32[1536]{0:T(1024)S(1)} collective-permute-done((f32[1536]{0:T(1024)S(1)}, f32[1536]{0:T(1024)S(1)}, u32[]{:S(2)}, u32[]{:S(2)}) %collective-permute-start.25) | collective-permute-done | bytes 6176 | tf_op jit(solution)/shard_map/ppermute | solution.py:26
  129.1 0.6 add_multiply_fusion
  129.7 0.0 collective-permute-done.20
  129.7 4.2 %fusion.2 = f32[1536,384]{1,0:T(8,128)} fusion(f32[1536,768]{1,0:T(8,128)} %copy-done.4, f32[1536,768]{1,0:T(8,128)} %copy-done.5, bf16[1536,384]{1,0:T(8,128)(2,1)S(1)} %collective-permute-done.20), kind=kLoop, calls=%fused_computation.5 | loop fusion | flops 2359296 | bytes 8257536 | tf_op jit(solution)/shard_map/mul | solution.py:217
  (17 shorter events, 0.1 us)
Async XLA Ops:
  0.8 1.0 copy-start
  1.7 0.7 copy-start.1
  2.4 0.7 copy-start.2
  3.1 0.7 copy-start.3
  5.3 15.7 %collective-permute-start.8 = (bf16[128,384]{1,0:T(8,128)(2,1)S(1)}, bf16[128,384]{1,0:T(8,128)(2,1)S(1)}, u32[]{:S(2)}, u32[]{:S(2)}) collective-permute-start(bf16[128,384]{1,0:T(8,128)(2,1)S(1)} %get-tuple-element.11), channel_id=1, source_target_pairs={{0,0},{128,96},{1,1},{129,97},{2,2},{130,98},{3,3},{131,99},{16,16... | collective-permute-start | bytes 294920 | tf_op jit(solution)/shard_map/ppermute | solution.py:26
  9.0 15.2 %collective-permute-start.9 = (bf16[128,384]{1,0:T(8,128)(2,1)S(1)}, bf16[128,384]{1,0:T(8,128)(2,1)S(1)}, u32[]{:S(2)}, u32[]{:S(2)}) collective-permute-start(bf16[128,384]{1,0:T(8,128)(2,1)S(1)} %get-tuple-element.12), channel_id=1, source_target_pairs={{0,1},{128,97},{1,2},{129,98},{2,3},{130,99},{3,0},{131,96},{16,17... | collective-permute-start | bytes 294920 | tf_op jit(solution)/shard_map/ppermute | solution.py:26
  12.9 13.2 %collective-permute-start.10 = (bf16[128,384]{1,0:T(8,128)(2,1)S(1)}, bf16[128,384]{1,0:T(8,128)(2,1)S(1)}, u32[]{:S(2)}, u32[]{:S(2)}) collective-permute-start(bf16[128,384]{1,0:T(8,128)(2,1)S(1)} %get-tuple-element.13), channel_id=1, source_target_pairs={{0,2},{128,98},{1,3},{129,99},{2,0},{130,96},{3,1},{131,97},{16,18... | collective-permute-start | bytes 294920 | tf_op jit(solution)/shard_map/ppermute | solution.py:26
  16.9 10.5 %collective-permute-start.11 = (bf16[128,384]{1,0:T(8,128)(2,1)S(1)}, bf16[128,384]{1,0:T(8,128)(2,1)S(1)}, u32[]{:S(2)}, u32[]{:S(2)}) collective-permute-start(bf16[128,384]{1,0:T(8,128)(2,1)S(1)} %get-tuple-element.14), channel_id=1, source_target_pairs={{0,3},{128,99},{1,0},{129,96},{2,1},{130,97},{3,2},{131,98},{16,19... | collective-permute-start | bytes 294920 | tf_op jit(solution)/shard_map/ppermute | solution.py:26
  21.0 10.9 %collective-permute-start.3 = (bf16[128,1536]{1,0:T(8,128)(2,1)S(1)}, bf16[128,1536]{1,0:T(8,128)(2,1)S(1)}, u32[]{:S(2)}, u32[]{:S(2)}) collective-permute-start(bf16[128,1536]{1,0:T(8,128)(2,1)S(1)} %get-tuple-element.10.refs_0_), channel_id=1, source_target_pairs={{0,128},{128,1},{1,129},{129,2},{2,130},{130,3},{3,131},{131,0},{1... | collective-permute-start | bytes 1179656 | tf_op jit(solution)/shard_map/ppermute | solution.py:26
  21.0 14.7 %collective-permute-start = (bf16[128,1536]{1,0:T(8,128)(2,1)S(1)}, bf16[128,1536]{1,0:T(8,128)(2,1)S(1)}, u32[]{:S(2)}, u32[]{:S(2)}) collective-permute-start(bf16[128,1536]{1,0:T(8,128)(2,1)S(1)} %get-tuple-element.10.refs_0_), channel_id=1, source_target_pairs={{0,131},{128,0},{1,128},{129,1},{2,129},{130,2},{3,130},{131,3},{1... | collective-permute-start | bytes 1179656 | tf_op jit(solution)/shard_map/ppermute | solution.py:26
  27.5 12.0 %collective-permute-start.12 = (bf16[4,128,384]{2,1,0:T(8,128)(2,1)S(1)}, bf16[4,128,384]{2,1,0:T(8,128)(2,1)S(1)}, u32[]{:S(2)}, u32[]{:S(2)}) collective-permute-start(bf16[4,128,384]{2,1,0:T(8,128)(2,1)S(1)} %pad_maximum_fusion.refs_9_), channel_id=1, source_target_pairs={{0,16},{128,144},{1,17},{129,145},{2,18},{130,146},{3,19},{131,147... | collective-permute-start | bytes 1179656 | tf_op jit(solution)/shard_map/ppermute | solution.py:26
  27.6 13.1 %collective-permute-start.13 = (bf16[4,128,384]{2,1,0:T(8,128)(2,1)S(1)}, bf16[4,128,384]{2,1,0:T(8,128)(2,1)S(1)}, u32[]{:S(2)}, u32[]{:S(2)}) collective-permute-start(bf16[4,128,384]{2,1,0:T(8,128)(2,1)S(1)} %pad_maximum_fusion.refs_9_), channel_id=1, source_target_pairs={{0,32},{128,160},{1,33},{129,161},{2,34},{130,162},{3,35},{131,163... | collective-permute-start | bytes 1179656 | tf_op jit(solution)/shard_map/ppermute | solution.py:26
  31.9 10.3 %collective-permute-start.4 = (bf16[128,1536]{1,0:T(8,128)(2,1)S(1)}, bf16[128,1536]{1,0:T(8,128)(2,1)S(1)}, u32[]{:S(2)}, u32[]{:S(2)}) collective-permute-start(bf16[128,1536]{1,0:T(8,128)(2,1)S(1)} %collective-permute-done.3.refs_8_), channel_id=1, source_target_pairs={{0,128},{128,1},{1,129},{129,2},{2,130},{130,3},{3,131},{131,0},{1... | collective-permute-start | bytes 1179656 | tf_op jit(solution)/shard_map/ppermute | solution.py:26
  35.7 12.2 %collective-permute-start.1 = (bf16[128,1536]{1,0:T(8,128)(2,1)S(1)}, bf16[128,1536]{1,0:T(8,128)(2,1)S(1)}, u32[]{:S(2)}, u32[]{:S(2)}) collective-permute-start(bf16[128,1536]{1,0:T(8,128)(2,1)S(1)} %collective-permute-done.refs_1_), channel_id=1, source_target_pairs={{0,131},{128,0},{1,128},{129,1},{2,129},{130,2},{3,130},{131,3},{1... | collective-permute-start | bytes 1179656 | tf_op jit(solution)/shard_map/ppermute | solution.py:26
  39.4 12.2 %collective-permute-start.14 = (bf16[4,128,384]{2,1,0:T(8,128)(2,1)S(1)}, bf16[4,128,384]{2,1,0:T(8,128)(2,1)S(1)}, u32[]{:S(2)}, u32[]{:S(2)}) collective-permute-start(bf16[4,128,384]{2,1,0:T(8,128)(2,1)S(1)} %collective-permute-done.12.refs_10_), channel_id=1, source_target_pairs={{0,32},{128,160},{1,33},{129,161},{2,34},{130,162},{3,35},{131,163... | collective-permute-start | bytes 1179656 | tf_op jit(solution)/shard_map/ppermute | solution.py:26
  40.7 11.5 %collective-permute-start.17 = (bf16[4,128,384]{2,1,0:T(8,128)(2,1)S(1)}, bf16[4,128,384]{2,1,0:T(8,128)(2,1)S(1)}, u32[]{:S(2)}, u32[]{:S(2)}) collective-permute-start(bf16[4,128,384]{2,1,0:T(8,128)(2,1)S(1)} %collective-permute-done.13.refs_11_), channel_id=1, source_target_pairs={{0,32},{128,160},{1,33},{129,161},{2,34},{130,162},{3,35},{131,163... | collective-permute-start | bytes 1179656 | tf_op jit(solution)/shard_map/ppermute | solution.py:26
  42.2 10.8 %collective-permute-start.5 = (bf16[128,1536]{1,0:T(8,128)(2,1)S(1)}, bf16[128,1536]{1,0:T(8,128)(2,1)S(1)}, u32[]{:S(2)}, u32[]{:S(2)}) collective-permute-start(bf16[128,1536]{1,0:T(8,128)(2,1)S(1)} %collective-permute-done.4.refs_7_), channel_id=1, source_target_pairs={{0,128},{128,1},{1,129},{129,2},{2,130},{130,3},{3,131},{131,0},{1... | collective-permute-start | bytes 1179656 | tf_op jit(solution)/shard_map/ppermute | solution.py:26
  48.0 11.4 %collective-permute-start.2 = (bf16[128,1536]{1,0:T(8,128)(2,1)S(1)}, bf16[128,1536]{1,0:T(8,128)(2,1)S(1)}, u32[]{:S(2)}, u32[]{:S(2)}) collective-permute-start(bf16[128,1536]{1,0:T(8,128)(2,1)S(1)} %collective-permute-done.1.refs_2_), channel_id=1, source_target_pairs={{0,131},{128,0},{1,128},{129,1},{2,129},{130,2},{3,130},{131,3},{1... | collective-permute-start | bytes 1179656 | tf_op jit(solution)/shard_map/ppermute | solution.py:26
  51.7 11.5 %collective-permute-start.15 = (bf16[4,128,384]{2,1,0:T(8,128)(2,1)S(1)}, bf16[4,128,384]{2,1,0:T(8,128)(2,1)S(1)}, u32[]{:S(2)}, u32[]{:S(2)}) collective-permute-start(bf16[4,128,384]{2,1,0:T(8,128)(2,1)S(1)} %collective-permute-done.13.refs_11_), channel_id=1, source_target_pairs={{0,16},{128,144},{1,17},{129,145},{2,18},{130,146},{3,19},{131,147... | collective-permute-start | bytes 1179656 | tf_op jit(solution)/shard_map/ppermute | solution.py:26
  51.7 11.5 %collective-permute-start.16 = (bf16[4,128,384]{2,1,0:T(8,128)(2,1)S(1)}, bf16[4,128,384]{2,1,0:T(8,128)(2,1)S(1)}, u32[]{:S(2)}, u32[]{:S(2)}) collective-permute-start(bf16[4,128,384]{2,1,0:T(8,128)(2,1)S(1)} %collective-permute-done.14.refs_12_), channel_id=1, source_target_pairs={{0,16},{128,144},{1,17},{129,145},{2,18},{130,146},{3,19},{131,147... | collective-permute-start | bytes 1179656 | tf_op jit(solution)/shard_map/ppermute | solution.py:26
  52.2 11.0 %collective-permute-start.18 = (bf16[4,128,384]{2,1,0:T(8,128)(2,1)S(1)}, bf16[4,128,384]{2,1,0:T(8,128)(2,1)S(1)}, u32[]{:S(2)}, u32[]{:S(2)}) collective-permute-start(bf16[4,128,384]{2,1,0:T(8,128)(2,1)S(1)} %collective-permute-done.17.refs_15_), channel_id=1, source_target_pairs={{0,16},{128,144},{1,17},{129,145},{2,18},{130,146},{3,19},{131,147... | collective-permute-start | bytes 1179656 | tf_op jit(solution)/shard_map/ppermute | solution.py:26
  53.1 10.1 %collective-permute-start.6 = (bf16[64,1536]{1,0:T(8,128)(2,1)S(1)}, bf16[64,1536]{1,0:T(8,128)(2,1)S(1)}, u32[]{:S(2)}, u32[]{:S(2)}) collective-permute-start(bf16[64,1536]{1,0:T(8,128)(2,1)S(1)} %slice.32), channel_id=1, source_target_pairs={{0,128},{128,1},{1,129},{129,2},{2,130},{130,3},{3,131},{131,0},{1... | collective-permute-start | bytes 589832 | tf_op jit(solution)/shard_map/ppermute | solution.py:26
  59.4 7.0 %collective-permute-start.7 = (bf16[64,1536]{1,0:T(8,128)(2,1)S(1)}, bf16[64,1536]{1,0:T(8,128)(2,1)S(1)}, u32[]{:S(2)}, u32[]{:S(2)}) collective-permute-start(bf16[64,1536]{1,0:T(8,128)(2,1)S(1)} %slice.33), channel_id=1, source_target_pairs={{0,131},{128,0},{1,128},{129,1},{2,129},{130,2},{3,130},{131,3},{1... | collective-permute-start | bytes 589832 | tf_op jit(solution)/shard_map/ppermute | solution.py:26
  70.5 28.9 %collective-permute-start.19 = (bf16[1536,768]{1,0:T(8,128)(2,1)S(1)}, bf16[1536,768]{1,0:T(8,128)(2,1)S(1)}, u32[]{:S(2)}, u32[]{:S(2)}) collective-permute-start(bf16[1536,768]{1,0:T(8,128)(2,1)S(1)} %convolution_convert_fusion), channel_id=1, source_target_pairs={{0,4},{128,132},{1,5},{129,133},{2,6},{130,134},{3,7},{131,135},{1... | collective-permute-start | bytes 7077896 | tf_op jit(solution)/shard_map/ppermute | solution.py:26
  74.7 25.0 %copy-start.5 = (f32[1536,768]{1,0:T(8,128)}, f32[1536,768]{1,0:T(8,128)S(1)}, u32[]{:S(2)}) copy-start(f32[1536,768]{1,0:T(8,128)S(1)} %fusion.4) | copy-start | bytes 14155780
  99.8 2.2 %copy-start.4 = (f32[1536,768]{1,0:T(8,128)}, f32[1536,768]{1,0:T(8,128)S(1)}, u32[]{:S(2)}) copy-start(f32[1536,768]{1,0:T(8,128)S(1)} %convert_element_type.13) | copy-start | bytes 14155780
  101.9 27.8 %collective-permute-start.20 = (bf16[1536,384]{1,0:T(8,128)(2,1)S(1)}, bf16[1536,384]{1,0:T(8,128)(2,1)S(1)}, u32[]{:S(2)}, u32[]{:S(2)}) collective-permute-start(bf16[1536,384]{1,0:T(8,128)(2,1)S(1)} %fusion), channel_id=1, source_target_pairs={{0,12},{128,140},{1,13},{129,141},{2,14},{130,142},{3,15},{131,143... | collective-permute-start | bytes 3538952 | tf_op jit(solution)/shard_map/ppermute | solution.py:26
  104.7 3.7 %collective-permute-start.21 = (f32[1536]{0:T(1024)S(1)}, f32[1536]{0:T(1024)S(1)}, u32[]{:S(2)}, u32[]{:S(2)}) collective-permute-start(f32[1536]{0:T(1024)S(1)} %reduce), channel_id=1, source_target_pairs={{0,128},{128,0},{1,129},{129,1},{2,130},{130,2},{3,131},{131,3},{1... | collective-permute-start | bytes 18440 | tf_op jit(solution)/shard_map/ppermute | solution.py:26
  108.5 4.6 %collective-permute-start.22 = (f32[1536]{0:T(1024)S(1)}, f32[1536]{0:T(1024)S(1)}, u32[]{:S(2)}, u32[]{:S(2)}) collective-permute-start(f32[1536]{0:T(1024)S(1)} %add.38), channel_id=1, source_target_pairs={{0,1},{128,129},{1,0},{129,128},{2,3},{130,131},{3,2},{131,130},{1... | collective-permute-start | bytes 18440 | tf_op jit(solution)/shard_map/ppermute | solution.py:26
  113.0 7.6 %collective-permute-start.23 = (f32[1536]{0:T(1024)S(1)}, f32[1536]{0:T(1024)S(1)}, u32[]{:S(2)}, u32[]{:S(2)}) collective-permute-start(f32[1536]{0:T(1024)S(1)} %add.39), channel_id=1, source_target_pairs={{0,2},{128,130},{1,3},{129,131},{2,0},{130,128},{3,1},{131,129},{1... | collective-permute-start | bytes 18440 | tf_op jit(solution)/shard_map/ppermute | solution.py:26
  120.6 4.9 %collective-permute-start.24 = (f32[1536]{0:T(1024)S(1)}, f32[1536]{0:T(1024)S(1)}, u32[]{:S(2)}, u32[]{:S(2)}) collective-permute-start(f32[1536]{0:T(1024)S(1)} %add.40), channel_id=1, source_target_pairs={{0,12},{128,140},{1,13},{129,141},{2,14},{130,142},{3,15},{131,143... | collective-permute-start | bytes 18440 | tf_op jit(solution)/shard_map/ppermute | solution.py:26
  125.4 3.7 %collective-permute-start.25 = (f32[1536]{0:T(1024)S(1)}, f32[1536]{0:T(1024)S(1)}, u32[]{:S(2)}, u32[]{:S(2)}) collective-permute-start(f32[1536]{0:T(1024)S(1)} %add.41), channel_id=1, source_target_pairs={{0,4},{128,132},{1,5},{129,133},{2,6},{130,134},{3,7},{131,135},{1... | collective-permute-start | bytes 18440 | tf_op jit(solution)/shard_map/ppermute | solution.py:26

commit v2 on v1

v2 whole, which is shorter than its diff:
```python
import jax
import jax.numpy as jnp
from jax import lax
from jax.experimental import pallas as pl
from jax.experimental.pallas import tpu as pltpu
from jax.sharding import PartitionSpec as P


AXES = ("arcs", "trow", "tcol")
CHUNKS = 1
VMEM = pl.BlockSpec(memory_space=pltpu.VMEM)
SMEM = pl.BlockSpec(memory_space=pltpu.SMEM)


def device_index(x, y, core, zh, zl):
    return (zl * 8 + y * 2 + core) * 16 + x * 4 + zh


def moved(value, where):
    pairs = []
    for x in range(4):
        for y in range(4):
            for core in range(2):
                for zh in range(4):
                    for zl in range(2):
                        pairs.append(
                            (device_index(x, y, core, zh, zl), device_index(*where(x, y, core, zh, zl)))
                        )
    return lax.ppermute(value, AXES, pairs)


def along_z(step):
    def where(x, y, core, zh, zl):
        z = (zh * 2 + zl + step) % 8
        return x, y, core, z // 2, z % 2

    return where


def round_y(x, y, core, zh, zl):
    return x, (y + (1 if core == 0 else 3)) % 4, core, zh, zl


def other_core(x, y, core, zh, zl):
    return x, y, 1 - core, zh, zl


def first_x(x, y, core, zh, zl):
    return x ^ (1 if core == 0 else 3), y, core, zh, zl


def second_x(x, y, core, zh, zl):
    return x ^ (3 if core == 0 else 1), y, core, zh, zl


def flip_z(mask):
    def where(x, y, core, zh, zl):
        z = (zh * 2 + zl) ^ mask
        return x, y, core, z // 2, z % 2

    return where


def to_share(turn):
    def where(x, y, core, zh, zl):
        a = y // 2
        return x, (y if zl == a else 3 - y), core, (zh + turn) % 4, a

    return where


def centre(where_ref, design_ref, small_ref, *refs):
    chunk_refs, share_refs = refs[:CHUNKS], refs[CHUNKS : CHUNKS + 4]
    rhs_ref, out_ref = refs[CHUNKS + 4 :]
    rows, cols = design_ref.shape
    arcs = (small_ref.shape[1] - rows) // 2
    length = rows // arcs
    slot = lax.broadcasted_iota(jnp.int32, (length, 1), 0).astype(jnp.float32)
    lane = lax.broadcasted_iota(jnp.int32, (1, rows), 1).astype(jnp.float32)
    observed = small_ref[:, :rows]
    weighted = jnp.zeros((1, rows), jnp.float32)
    for arc in range(arcs):
        root = jnp.sqrt(small_ref[:, rows + arc : rows + arc + 1])
        count = small_ref[:, rows + arcs + arc : rows + arcs + arc + 1]
        mask = (slot < count).astype(jnp.float32)
        piece = design_ref[pl.ds(arc * length, length), :].astype(jnp.float32)
        mean = jnp.sum(mask * piece, axis=0, keepdims=True) / count
        out_ref[pl.ds(arc * length, length), :] = ((mask * root) * (piece - mean)).astype(jnp.bfloat16)
        inside = ((lane >= arc * length) & (lane < arc * length + count)).astype(jnp.float32)
        series_mean = jnp.sum(inside * observed, axis=1, keepdims=True) / count
        weighted = weighted + (inside * root) * (observed - series_mean)
    high = weighted.astype(jnp.bfloat16)
    rest1 = weighted - high.astype(jnp.float32)
    middle = rest1.astype(jnp.bfloat16)
    low = (rest1 - middle.astype(jnp.float32)).astype(jnp.bfloat16)
    row = lax.broadcasted_iota(jnp.int32, (8, rows), 0)
    parts = jnp.where(
        row == 0,
        high.astype(jnp.float32),
        jnp.where(row == 1, middle.astype(jnp.float32), jnp.where(row == 2, low.astype(jnp.float32), 0.0)),
    ).astype(jnp.bfloat16)
    sums = jnp.dot(parts, out_ref[...], preferred_element_type=jnp.float32)
    rhs_ref[...] = jnp.sum(sums, axis=0, keepdims=True)
    narrow = cols // 4
    for turn, share_ref in enumerate(share_refs):
        start = pl.multiple_of(((where_ref[3] + turn) % 4) * narrow, 128)
        share_ref[...] = out_ref[:, pl.ds(start, narrow)]
    wide = cols // CHUNKS
    for c, chunk_ref in enumerate(chunk_refs):
        chunk_ref[...] = out_ref[:, c * wide : (c + 1) * wide]


def joined(columns):
    rows = sum(piece.shape[0] for piece in columns[0])
    wide = sum(pieces[0].shape[-1] for pieces in columns)

    def join(*refs):
        refs, out_ref, left = iter(refs[:-1]), refs[-1], 0
        for pieces in columns:
            top = 0
            for piece in pieces:
                spot = (pl.ds(top, piece.shape[0]),) + (slice(None),) * (piece.ndim - 2)
                out_ref[spot + (pl.ds(left, piece.shape[-1]),)] = next(refs)[...]
                top += piece.shape[0]
            left += pieces[0].shape[-1]

    flat = [piece for pieces in columns for piece in pieces]
    return pl.pallas_call(
        join,
        out_shape=jax.ShapeDtypeStruct((rows, *flat[0].shape[1:-1], wide), flat[0].dtype),
        in_specs=[VMEM] * len(flat),
        out_specs=VMEM,
        compiler_params=pltpu.CompilerParams(vmem_limit_bytes=12 << 20),
    )(*flat)


def place(where_ref, mine_ref, theirs_ref, cols_out):
    x, y, core, zh, zl = (where_ref[i] for i in range(5))
    z = 2 * zh + zl
    first = jnp.where(core == 0, 1, 3)
    for other, ref in enumerate((mine_ref, theirs_ref)):
        source_core = (core + other) % 2
        for step in range(4):
            from_y = (y + jnp.where(source_core == 0, 4 - step, step)) % 4
            near = from_y // 2 == zl
            of_y = jnp.where(near, from_y, 3 - from_y)
            of_zl = jnp.where(near, zl, 1 - zl)
            m = (2 * (of_y % 2) + source_core) ^ x
            spot = jnp.where(m == 0, 0, jnp.where(m == 2, 3, jnp.where(m == first, 2, 1)))
            for turn in range(4):
                of_z = 2 * ((zh + 4 - turn) % 4) + of_zl
                ahead = (of_z + 8 - z) % 8
                cols_out[spot, pl.ds(pl.multiple_of(ahead * 128, 128), 128), :] = ref[4 * step + turn]


def product(left, right):
    return lax.dot_general(left, right, (((0,), (0,)), ((), ())), preferred_element_type=jnp.float32)


def local(design, observed, arc_counts, arc_weight):
    rows, cols = design.shape
    narrow = cols // 4
    obs_total = 4096
    bf16, f32 = jnp.bfloat16, jnp.float32
    trow, tcol = lax.axis_index("trow"), lax.axis_index("tcol")
    where = jnp.stack([tcol // 4, trow // 2, trow % 2, tcol % 4, lax.axis_index("arcs")])

    small = jnp.concatenate([observed, arc_weight, arc_counts.astype(f32)])
    out = pl.pallas_call(
        centre,
        out_shape=[jax.ShapeDtypeStruct((rows, cols // CHUNKS), bf16)] * CHUNKS
        + [jax.ShapeDtypeStruct((rows, narrow), bf16)] * 4
        + [jax.ShapeDtypeStruct((1, cols), f32)],
        in_specs=[SMEM, VMEM, VMEM],
        out_specs=[VMEM] * (CHUNKS + 5),
        scratch_shapes=[pltpu.VMEM((rows, cols), bf16)],
        compiler_params=pltpu.CompilerParams(vmem_limit_bytes=8 << 20),
        name="centre",
    )(where, design, small.reshape(1, -1))
    own, shares, rhs = out[:CHUNKS], out[CHUNKS:-1], out[-1].reshape(cols)

    mine = [jnp.concatenate([moved(shares[turn], to_share(turn))[None] for turn in range(4)])]
    for _ in range(1, 4):
        mine.append(moved(mine[-1], round_y))
    mine = joined([mine])
    theirs = moved(mine, other_core)
    right = pl.pallas_call(
        place,
        out_shape=jax.ShapeDtypeStruct((4, 8 * rows, narrow), bf16),
        in_specs=[SMEM, VMEM, VMEM],
        out_specs=VMEM,
        compiler_params=pltpu.CompilerParams(vmem_limit_bytes=12 << 20),
        name="place",
    )(where, mine, theirs)

    half = rows // 2
    columns = []
    for piece in own:
        up, down = [piece], [piece]
        for _ in range(1, 4):
            up.append(moved(up[-1], along_z(1)))
            down.append(moved(down[-1], along_z(-1)))
        far = [moved(up[3][:half], along_z(1)), moved(down[3][half:], along_z(-1))]
        columns.append([piece, *down[1:], *far, up[3], up[2], up[1]])
    left = joined(columns)

    far = moved(product(left, right[3]).astype(bf16), first_x)
    near = moved(product(left, right[2]).astype(bf16), first_x)
    second, tile = lax.optimization_barrier((product(left, right[1]), product(left, right[0])))
    last = moved((second + far.astype(f32)).astype(bf16), second_x)
    gram = (tile + near.astype(f32) + last.astype(f32)) * (1.0 / obs_total)

    rhs = rhs + moved(rhs, first_x)
    rhs = rhs + moved(rhs, second_x)
    for mask in (1, 2, 4):
        rhs = rhs + moved(rhs, flip_z(mask))
    return (gram, rhs * obs_total ** (-0.5))


def solution(mesh):
    return jax.shard_map(
        local,
        mesh=mesh,
        in_specs=(
            P(("arcs", "tcol"), "trow"),
            P(("arcs", "tcol")),
            P(("arcs", "tcol")),
            P(("arcs", "tcol")),
        ),
        out_specs=(P("trow", ("arcs", "tcol")), P("trow")),
        check_vma=False,
    )
```

time: 134 us -> 168 us (1.25)
  the two profiles are of different devices: /device:TPU:16 before, /device:TPU:6 now
where the time goes in v2:
time: 168 us
  waiting for transfers between devices  109 us (65%)
  starting transfers between devices  39.2 us (23%)
  matrix products  8.39 us (5%)
  other arithmetic  6.51 us (4%)
  Pallas kernels  2.36 us (1%)
    ppermute x24, waiting for transfers between devices, moved(): return lax.ppermute(value, AXES, pairs)  109 us
    ppermute x24, starting transfers between devices, moved(): return lax.ppermute(value, AXES, pairs)  39.2 us
    dot_general x4, matrix products, product(): lax.dot_general(left, right, (((0,), (0,)), ((), ())), preferred_element_...  8.39 us
  transfers between devices with their start and end apart: 24, of which 14 were waited for; matrix products, arithmetic and copies ran while one was open for 5% of the time, Pallas kernels for 0%

profile of v2, /device:TPU:6, one launch (start us, length us, event | category | flops | bytes accessed | tf_op | source)
XLA Modules:
  0.0 167.7 jit_solution(7100925474749456507)
XLA Ops:
  0.7 0.7 convert_element_type.21
  1.3 0.7 pad_maximum_fusion.1
  2.1 0.1 stack.23.where_ref
  2.2 1.0 copy-done
  3.2 1.0 centre.1
  4.2 0.7 collective-permute-start.8
  4.9 3.4 %collective-permute-start.9 = (bf16[128,384]{1,0:T(8,128)(2,1)S(1)}, bf16[128,384]{1,0:T(8,128)(2,1)S(1)}, u32[]{:S(2)}, u32[]{:S(2)}) collective-permute-start(bf16[128,384]{1,0:T(8,128)(2,1)S(1)} %get-tuple-element.12), channel_id=1, source_target_pairs={{0,1},{128,97},{1,2},{129,98},{2,3},{130,99},{3,0},{131,96},{16,17... | collective-permute-start | bytes 294920 | tf_op jit(solution)/shard_map/ppermute | solution.py:29
  8.2 5.4 %collective-permute-start.10 = (bf16[128,384]{1,0:T(8,128)(2,1)S(1)}, bf16[128,384]{1,0:T(8,128)(2,1)S(1)}, u32[]{:S(2)}, u32[]{:S(2)}) collective-permute-start(bf16[128,384]{1,0:T(8,128)(2,1)S(1)} %get-tuple-element.13), channel_id=1, source_target_pairs={{0,2},{128,98},{1,3},{129,99},{2,0},{130,96},{3,1},{131,97},{16,18... | collective-permute-start | bytes 294920 | tf_op jit(solution)/shard_map/ppermute | solution.py:29
  13.6 2.7 %collective-permute-start.11 = (bf16[128,384]{1,0:T(8,128)(2,1)S(1)}, bf16[128,384]{1,0:T(8,128)(2,1)S(1)}, u32[]{:S(2)}, u32[]{:S(2)}) collective-permute-start(bf16[128,384]{1,0:T(8,128)(2,1)S(1)} %get-tuple-element.14), channel_id=1, source_target_pairs={{0,3},{128,99},{1,0},{129,96},{2,1},{130,97},{3,2},{131,98},{16,19... | collective-permute-start | bytes 294920 | tf_op jit(solution)/shard_map/ppermute | solution.py:29
  16.3 0.0 collective-permute-done.8
  16.3 0.0 collective-permute-done.9
  16.3 3.2 %collective-permute-done.10 = bf16[128,384]{1,0:T(8,128)(2,1)S(1)} collective-permute-done((bf16[128,384]{1,0:T(8,128)(2,1)S(1)}, bf16[128,384]{1,0:T(8,128)(2,1)S(1)}, u32[]{:S(2)}, u32[]{:S(2)}) %collective-permute-start.10) | collective-permute-done | bytes 98336 | tf_op jit(solution)/shard_map/ppermute | solution.py:29
  19.4 0.0 collective-permute-done.11
  19.4 0.1 pad_maximum_fusion.refs_0_
  19.5 1.6 collective-permute-start.12
  21.1 14.1 %collective-permute-done.12.refs_1_ = bf16[4,128,384]{2,1,0:T(8,128)(2,1)S(1)} collective-permute-done((bf16[4,128,384]{2,1,0:T(8,128)(2,1)S(1)}, bf16[4,128,384]{2,1,0:T(8,128)(2,1)S(1)}, u32[]{:S(2)}, u32[]{:S(2)}) %collective-permute-start.12) | collective-permute-done | bytes 393248 | tf_op jit(solution)/shard_map/ppermute | solution.py:29
  35.2 0.0 collective-permute-start.13
  35.2 9.0 %collective-permute-done.13.refs_2_ = bf16[4,128,384]{2,1,0:T(8,128)(2,1)S(1)} collective-permute-done((bf16[4,128,384]{2,1,0:T(8,128)(2,1)S(1)}, bf16[4,128,384]{2,1,0:T(8,128)(2,1)S(1)}, u32[]{:S(2)}, u32[]{:S(2)}) %collective-permute-start.13) | collective-permute-done | bytes 393248 | tf_op jit(solution)/shard_map/ppermute | solution.py:29
  44.2 0.0 collective-permute-start.14
  44.2 9.0 %collective-permute-done.14.refs_3_ = bf16[4,128,384]{2,1,0:T(8,128)(2,1)S(1)} collective-permute-done((bf16[4,128,384]{2,1,0:T(8,128)(2,1)S(1)}, bf16[4,128,384]{2,1,0:T(8,128)(2,1)S(1)}, u32[]{:S(2)}, u32[]{:S(2)}) %collective-permute-start.14) | collective-permute-done | bytes 393248 | tf_op jit(solution)/shard_map/ppermute | solution.py:29
  53.1 0.1 shard_map.60.mine_ref
  53.3 0.1 collective-permute-start.15
  53.4 4.3 %collective-permute-start.3 = (bf16[128,1536]{1,0:T(8,128)(2,1)S(1)}, bf16[128,1536]{1,0:T(8,128)(2,1)S(1)}, u32[]{:S(2)}, u32[]{:S(2)}) collective-permute-start(bf16[128,1536]{1,0:T(8,128)(2,1)S(1)} %get-tuple-element.10.refs_0_), channel_id=1, source_target_pairs={{0,128},{128,1},{1,129},{129,2},{2,130},{130,3},{3,131},{131,0},{1... | collective-permute-start | bytes 1179656 | tf_op jit(solution)/shard_map/ppermute | solution.py:29
  57.7 2.2 %collective-permute-start = (bf16[128,1536]{1,0:T(8,128)(2,1)S(1)}, bf16[128,1536]{1,0:T(8,128)(2,1)S(1)}, u32[]{:S(2)}, u32[]{:S(2)}) collective-permute-start(bf16[128,1536]{1,0:T(8,128)(2,1)S(1)} %get-tuple-element.10.refs_0_), channel_id=1, source_target_pairs={{0,131},{128,0},{1,128},{129,1},{2,129},{130,2},{3,130},{131,3},{1... | collective-permute-start | bytes 1179656 | tf_op jit(solution)/shard_map/ppermute | solution.py:29
  59.8 9.6 %collective-permute-done.3.refs_8_ = bf16[128,1536]{1,0:T(8,128)(2,1)S(1)} collective-permute-done((bf16[128,1536]{1,0:T(8,128)(2,1)S(1)}, bf16[128,1536]{1,0:T(8,128)(2,1)S(1)}, u32[]{:S(2)}, u32[]{:S(2)}) %collective-permute-start.3) | collective-permute-done | bytes 393248 | tf_op jit(solution)/shard_map/ppermute | solution.py:29
  69.5 0.0 collective-permute-start.4
  69.5 0.0 collective-permute-done.refs_1_
  69.5 3.2 %collective-permute-start.1 = (bf16[128,1536]{1,0:T(8,128)(2,1)S(1)}, bf16[128,1536]{1,0:T(8,128)(2,1)S(1)}, u32[]{:S(2)}, u32[]{:S(2)}) collective-permute-start(bf16[128,1536]{1,0:T(8,128)(2,1)S(1)} %collective-permute-done.refs_1_), channel_id=1, source_target_pairs={{0,131},{128,0},{1,128},{129,1},{2,129},{130,2},{3,130},{131,3},{1... | collective-permute-start | bytes 1179656 | tf_op jit(solution)/shard_map/ppermute | solution.py:29
  72.7 8.8 %collective-permute-done.4.refs_7_ = bf16[128,1536]{1,0:T(8,128)(2,1)S(1)} collective-permute-done((bf16[128,1536]{1,0:T(8,128)(2,1)S(1)}, bf16[128,1536]{1,0:T(8,128)(2,1)S(1)}, u32[]{:S(2)}, u32[]{:S(2)}) %collective-permute-start.4) | collective-permute-done | bytes 393248 | tf_op jit(solution)/shard_map/ppermute | solution.py:29
  81.5 0.0 collective-permute-start.5
  81.5 0.0 collective-permute-done.1.refs_2_
  81.5 3.2 %collective-permute-start.2 = (bf16[128,1536]{1,0:T(8,128)(2,1)S(1)}, bf16[128,1536]{1,0:T(8,128)(2,1)S(1)}, u32[]{:S(2)}, u32[]{:S(2)}) collective-permute-start(bf16[128,1536]{1,0:T(8,128)(2,1)S(1)} %collective-permute-done.1.refs_2_), channel_id=1, source_target_pairs={{0,131},{128,0},{1,128},{129,1},{2,129},{130,2},{3,130},{131,3},{1... | collective-permute-start | bytes 1179656 | tf_op jit(solution)/shard_map/ppermute | solution.py:29
  84.8 8.0 %collective-permute-done.5.refs_6_ = bf16[128,1536]{1,0:T(8,128)(2,1)S(1)} collective-permute-done((bf16[128,1536]{1,0:T(8,128)(2,1)S(1)}, bf16[128,1536]{1,0:T(8,128)(2,1)S(1)}, u32[]{:S(2)}, u32[]{:S(2)}) %collective-permute-start.5) | collective-permute-done | bytes 393248 | tf_op jit(solution)/shard_map/ppermute | solution.py:29
  92.8 0.1 collective-permute-start.6
  92.9 0.0 collective-permute-done.2.refs_3_
  92.9 3.5 %collective-permute-start.7 = (bf16[64,1536]{1,0:T(8,128)(2,1)S(1)}, bf16[64,1536]{1,0:T(8,128)(2,1)S(1)}, u32[]{:S(2)}, u32[]{:S(2)}) collective-permute-start(bf16[64,1536]{1,0:T(8,128)(2,1)S(1)} %slice.25), channel_id=1, source_target_pairs={{0,131},{128,0},{1,128},{129,1},{2,129},{130,2},{3,130},{131,3},{1... | collective-permute-start | bytes 589832 | tf_op jit(solution)/shard_map/ppermute | solution.py:29
  96.4 3.4 %collective-permute-done.6.refs_4_ = bf16[64,1536]{1,0:T(8,128)(2,1)S(1)} collective-permute-done((bf16[64,1536]{1,0:T(8,128)(2,1)S(1)}, bf16[64,1536]{1,0:T(8,128)(2,1)S(1)}, u32[]{:S(2)}, u32[]{:S(2)}) %collective-permute-start.6) | collective-permute-done | bytes 196640 | tf_op jit(solution)/shard_map/ppermute | solution.py:29
  99.7 0.0 collective-permute-done.7.refs_5_
  99.7 0.2 shard_map.59
  99.9 0.0 collective-permute-done.15.theirs_ref
  99.9 1.0 place.1
  100.9 1.8 %convolution_convert_fusion = bf16[1536,384]{1,0:T(8,128)(2,1)S(1)} fusion(bf16[1024,1536]{1,0:T(8,128)(2,1)S(1)} %shard_map.59, bf16[4,1024,384]{2,1,0:T(8,128)(2,1)S(1)} %place.1), kind=kOutput, calls=%fused_computation | convolution fusion | flops 1208549376 | bytes 5111808 | tf_op jit(solution)/shard_map/dot_general | solution.py:157
  102.8 0.9 collective-permute-start.17
  103.7 2.9 %convolution_convert_fusion.1 = bf16[1536,384]{1,0:T(8,128)(2,1)} fusion(bf16[1024,1536]{1,0:T(8,128)(2,1)S(1)} %shard_map.59, bf16[4,1024,384]{2,1,0:T(8,128)(2,1)S(1)} %place.1), kind=kOutput, calls=%fused_computation.1 | convolution fusion | flops 1208549376 | bytes 5111808 | tf_op jit(solution)/shard_map/dot_general | solution.py:157
  106.6 1.2 collective-permute-start.16
  107.8 1.8 %fusion = f32[1536,384]{1,0:T(8,128)S(1)} fusion(bf16[1024,1536]{1,0:T(8,128)(2,1)S(1)} %shard_map.59, bf16[4,1024,384]{2,1,0:T(8,128)(2,1)S(1)} %place.1), kind=kOutput, calls=%fused_computation.7 | convolution fusion | flops 1207959552 | bytes 6291456 | tf_op jit(solution)/shard_map/dot_general | solution.py:157
  109.6 1.8 %fusion.1 = f32[1536,384]{1,0:T(8,128)S(1)} fusion(bf16[1024,1536]{1,0:T(8,128)(2,1)S(1)} %shard_map.59, bf16[4,1024,384]{2,1,0:T(8,128)(2,1)S(1)} %place.1), kind=kOutput, calls=%fused_computation.9 | convolution fusion | flops 1207959552 | bytes 6291456 | tf_op jit(solution)/shard_map/dot_general | solution.py:157
  111.5 7.6 %collective-permute-done.17 = bf16[1536,384]{1,0:T(8,128)(2,1)S(1)} collective-permute-done((bf16[1536,384]{1,0:T(8,128)(2,1)S(1)}, bf16[1536,384]{1,0:T(8,128)(2,1)S(1)}, u32[]{:S(2)}, u32[]{:S(2)}) %collective-permute-start.17) | collective-permute-done | bytes 1179680 | tf_op jit(solution)/shard_map/ppermute | solution.py:29
  119.1 1.3 add_convert_fusion
  120.4 0.5 collective-permute-start.18
  120.9 1.0 collective-permute-start.19
  121.8 21.5 %collective-permute-done.19 = f32[1536]{0:T(1024)S(1)} collective-permute-done((f32[1536]{0:T(1024)S(1)}, f32[1536]{0:T(1024)S(1)}, u32[]{:S(2)}, u32[]{:S(2)}) %collective-permute-start.19) | collective-permute-done | bytes 6176 | tf_op jit(solution)/shard_map/ppermute | solution.py:29
  143.4 0.5 collective-permute-start.20
  143.9 4.4 %collective-permute-done.20 = f32[1536]{0:T(1024)S(1)} collective-permute-done((f32[1536]{0:T(1024)S(1)}, f32[1536]{0:T(1024)S(1)}, u32[]{:S(2)}, u32[]{:S(2)}) %collective-permute-start.20) | collective-permute-done | bytes 6176 | tf_op jit(solution)/shard_map/ppermute | solution.py:29
  148.3 0.0 collective-permute-start.21
  148.3 3.6 %collective-permute-done.21 = f32[1536]{0:T(1024)S(1)} collective-permute-done((f32[1536]{0:T(1024)S(1)}, f32[1536]{0:T(1024)S(1)}, u32[]{:S(2)}, u32[]{:S(2)}) %collective-permute-start.21) | collective-permute-done | bytes 6176 | tf_op jit(solution)/shard_map/ppermute | solution.py:29
  151.9 2.2 %collective-permute-start.22 = (f32[1536]{0:T(1024)S(1)}, f32[1536]{0:T(1024)S(1)}, u32[]{:S(2)}, u32[]{:S(2)}) collective-permute-start(f32[1536]{0:T(1024)S(1)} %add.40), channel_id=1, source_target_pairs={{0,1},{128,129},{1,0},{129,128},{2,3},{130,131},{3,2},{131,130},{1... | collective-permute-start | bytes 18440 | tf_op jit(solution)/shard_map/ppermute | solution.py:29
  154.1 2.4 %collective-permute-done.22 = f32[1536]{0:T(1024)S(1)} collective-permute-done((f32[1536]{0:T(1024)S(1)}, f32[1536]{0:T(1024)S(1)}, u32[]{:S(2)}, u32[]{:S(2)}) %collective-permute-start.22) | collective-permute-done | bytes 6176 | tf_op jit(solution)/shard_map/ppermute | solution.py:29
  156.5 2.7 %collective-permute-start.23 = (f32[1536]{0:T(1024)S(1)}, f32[1536]{0:T(1024)S(1)}, u32[]{:S(2)}, u32[]{:S(2)}) collective-permute-start(f32[1536]{0:T(1024)S(1)} %add.41), channel_id=1, source_target_pairs={{0,2},{128,130},{1,3},{129,131},{2,0},{130,128},{3,1},{131,129},{1... | collective-permute-start | bytes 18440 | tf_op jit(solution)/shard_map/ppermute | solution.py:29
  159.1 4.9 %collective-permute-done.23 = f32[1536]{0:T(1024)S(1)} collective-permute-done((f32[1536]{0:T(1024)S(1)}, f32[1536]{0:T(1024)S(1)}, u32[]{:S(2)}, u32[]{:S(2)}) %collective-permute-start.23) | collective-permute-done | bytes 6176 | tf_op jit(solution)/shard_map/ppermute | solution.py:29
  164.0 0.6 add_multiply_fusion.1
  164.6 0.0 collective-permute-done.16
  164.6 0.0 collective-permute-done.18
  164.6 3.1 %add_multiply_fusion = f32[1536,384]{1,0:T(8,128)} fusion(bf16[1536,384]{1,0:T(8,128)(2,1)} %collective-permute-done.18, f32[1536,384]{1,0:T(8,128)S(1)} %fusion, bf16[1536,384]{1,0:T(8,128)(2,1)S(1)} %collective-permute-done.16), kind=kLoop, calls=%fused_computation.2 | loop fusion | flops 2949120 | bytes 7077888 | tf_op jit(solution)/shard_map/mul | solution.py:211
  (8 shorter events, 0.1 us)
Async XLA Ops:
  2.2 1.0 copy-start
  4.2 12.1 %collective-permute-start.8 = (bf16[128,384]{1,0:T(8,128)(2,1)S(1)}, bf16[128,384]{1,0:T(8,128)(2,1)S(1)}, u32[]{:S(2)}, u32[]{:S(2)}) collective-permute-start(bf16[128,384]{1,0:T(8,128)(2,1)S(1)} %get-tuple-element.11), channel_id=1, source_target_pairs={{0,0},{128,96},{1,1},{129,97},{2,2},{130,98},{3,3},{131,99},{16,16... | collective-permute-start | bytes 294920 | tf_op jit(solution)/shard_map/ppermute | solution.py:29
  4.9 11.4 %collective-permute-start.9 = (bf16[128,384]{1,0:T(8,128)(2,1)S(1)}, bf16[128,384]{1,0:T(8,128)(2,1)S(1)}, u32[]{:S(2)}, u32[]{:S(2)}) collective-permute-start(bf16[128,384]{1,0:T(8,128)(2,1)S(1)} %get-tuple-element.12), channel_id=1, source_target_pairs={{0,1},{128,97},{1,2},{129,98},{2,3},{130,99},{3,0},{131,96},{16,17... | collective-permute-start | bytes 294920 | tf_op jit(solution)/shard_map/ppermute | solution.py:29
  8.2 11.2 %collective-permute-start.10 = (bf16[128,384]{1,0:T(8,128)(2,1)S(1)}, bf16[128,384]{1,0:T(8,128)(2,1)S(1)}, u32[]{:S(2)}, u32[]{:S(2)}) collective-permute-start(bf16[128,384]{1,0:T(8,128)(2,1)S(1)} %get-tuple-element.13), channel_id=1, source_target_pairs={{0,2},{128,98},{1,3},{129,99},{2,0},{130,96},{3,1},{131,97},{16,18... | collective-permute-start | bytes 294920 | tf_op jit(solution)/shard_map/ppermute | solution.py:29
  13.6 5.8 %collective-permute-start.11 = (bf16[128,384]{1,0:T(8,128)(2,1)S(1)}, bf16[128,384]{1,0:T(8,128)(2,1)S(1)}, u32[]{:S(2)}, u32[]{:S(2)}) collective-permute-start(bf16[128,384]{1,0:T(8,128)(2,1)S(1)} %get-tuple-element.14), channel_id=1, source_target_pairs={{0,3},{128,99},{1,0},{129,96},{2,1},{130,97},{3,2},{131,98},{16,19... | collective-permute-start | bytes 294920 | tf_op jit(solution)/shard_map/ppermute | solution.py:29
  19.5 15.7 %collective-permute-start.12 = (bf16[4,128,384]{2,1,0:T(8,128)(2,1)S(1)}, bf16[4,128,384]{2,1,0:T(8,128)(2,1)S(1)}, u32[]{:S(2)}, u32[]{:S(2)}) collective-permute-start(bf16[4,128,384]{2,1,0:T(8,128)(2,1)S(1)} %pad_maximum_fusion.refs_0_), channel_id=1, source_target_pairs={{0,32},{128,160},{1,33},{129,161},{2,34},{130,162},{3,35},{131,163... | collective-permute-start | bytes 1179656 | tf_op jit(solution)/shard_map/ppermute | solution.py:29
  35.2 9.0 %collective-permute-start.13 = (bf16[4,128,384]{2,1,0:T(8,128)(2,1)S(1)}, bf16[4,128,384]{2,1,0:T(8,128)(2,1)S(1)}, u32[]{:S(2)}, u32[]{:S(2)}) collective-permute-start(bf16[4,128,384]{2,1,0:T(8,128)(2,1)S(1)} %collective-permute-done.12.refs_1_), channel_id=1, source_target_pairs={{0,32},{128,160},{1,33},{129,161},{2,34},{130,162},{3,35},{131,163... | collective-permute-start | bytes 1179656 | tf_op jit(solution)/shard_map/ppermute | solution.py:29
  44.2 9.0 %collective-permute-start.14 = (bf16[4,128,384]{2,1,0:T(8,128)(2,1)S(1)}, bf16[4,128,384]{2,1,0:T(8,128)(2,1)S(1)}, u32[]{:S(2)}, u32[]{:S(2)}) collective-permute-start(bf16[4,128,384]{2,1,0:T(8,128)(2,1)S(1)} %collective-permute-done.13.refs_2_), channel_id=1, source_target_pairs={{0,32},{128,160},{1,33},{129,161},{2,34},{130,162},{3,35},{131,163... | collective-permute-start | bytes 1179656 | tf_op jit(solution)/shard_map/ppermute | solution.py:29
  53.3 46.6 %collective-permute-start.15 = (bf16[16,128,384]{2,1,0:T(8,128)(2,1)S(1)}, bf16[16,128,384]{2,1,0:T(8,128)(2,1)S(1)}, u32[]{:S(2)}, u32[]{:S(2)}) collective-permute-start(bf16[16,128,384]{2,1,0:T(8,128)(2,1)S(1)} %shard_map.60.mine_ref), channel_id=1, source_target_pairs={{0,16},{128,144},{1,17},{129,145},{2,18},{130,146},{3,19},{131,147... | collective-permute-start | bytes 4718600 | tf_op jit(solution)/shard_map/ppermute | solution.py:29
  53.4 16.1 %collective-permute-start.3 = (bf16[128,1536]{1,0:T(8,128)(2,1)S(1)}, bf16[128,1536]{1,0:T(8,128)(2,1)S(1)}, u32[]{:S(2)}, u32[]{:S(2)}) collective-permute-start(bf16[128,1536]{1,0:T(8,128)(2,1)S(1)} %get-tuple-element.10.refs_0_), channel_id=1, source_target_pairs={{0,128},{128,1},{1,129},{129,2},{2,130},{130,3},{3,131},{131,0},{1... | collective-permute-start | bytes 1179656 | tf_op jit(solution)/shard_map/ppermute | solution.py:29
  57.7 11.8 %collective-permute-start = (bf16[128,1536]{1,0:T(8,128)(2,1)S(1)}, bf16[128,1536]{1,0:T(8,128)(2,1)S(1)}, u32[]{:S(2)}, u32[]{:S(2)}) collective-permute-start(bf16[128,1536]{1,0:T(8,128)(2,1)S(1)} %get-tuple-element.10.refs_0_), channel_id=1, source_target_pairs={{0,131},{128,0},{1,128},{129,1},{2,129},{130,2},{3,130},{131,3},{1... | collective-permute-start | bytes 1179656 | tf_op jit(solution)/shard_map/ppermute | solution.py:29
  69.5 12.1 %collective-permute-start.4 = (bf16[128,1536]{1,0:T(8,128)(2,1)S(1)}, bf16[128,1536]{1,0:T(8,128)(2,1)S(1)}, u32[]{:S(2)}, u32[]{:S(2)}) collective-permute-start(bf16[128,1536]{1,0:T(8,128)(2,1)S(1)} %collective-permute-done.3.refs_8_), channel_id=1, source_target_pairs={{0,128},{128,1},{1,129},{129,2},{2,130},{130,3},{3,131},{131,0},{1... | collective-permute-start | bytes 1179656 | tf_op jit(solution)/shard_map/ppermute | solution.py:29
  69.5 12.1 %collective-permute-start.1 = (bf16[128,1536]{1,0:T(8,128)(2,1)S(1)}, bf16[128,1536]{1,0:T(8,128)(2,1)S(1)}, u32[]{:S(2)}, u32[]{:S(2)}) collective-permute-start(bf16[128,1536]{1,0:T(8,128)(2,1)S(1)} %collective-permute-done.refs_1_), channel_id=1, source_target_pairs={{0,131},{128,0},{1,128},{129,1},{2,129},{130,2},{3,130},{131,3},{1... | collective-permute-start | bytes 1179656 | tf_op jit(solution)/shard_map/ppermute | solution.py:29
  81.5 11.2 %collective-permute-start.5 = (bf16[128,1536]{1,0:T(8,128)(2,1)S(1)}, bf16[128,1536]{1,0:T(8,128)(2,1)S(1)}, u32[]{:S(2)}, u32[]{:S(2)}) collective-permute-start(bf16[128,1536]{1,0:T(8,128)(2,1)S(1)} %collective-permute-done.4.refs_7_), channel_id=1, source_target_pairs={{0,128},{128,1},{1,129},{129,2},{2,130},{130,3},{3,131},{131,0},{1... | collective-permute-start | bytes 1179656 | tf_op jit(solution)/shard_map/ppermute | solution.py:29
  81.5 11.3 %collective-permute-start.2 = (bf16[128,1536]{1,0:T(8,128)(2,1)S(1)}, bf16[128,1536]{1,0:T(8,128)(2,1)S(1)}, u32[]{:S(2)}, u32[]{:S(2)}) collective-permute-start(bf16[128,1536]{1,0:T(8,128)(2,1)S(1)} %collective-permute-done.1.refs_2_), channel_id=1, source_target_pairs={{0,131},{128,0},{1,128},{129,1},{2,129},{130,2},{3,130},{131,3},{1... | collective-permute-start | bytes 1179656 | tf_op jit(solution)/shard_map/ppermute | solution.py:29
  92.8 7.0 %collective-permute-start.6 = (bf16[64,1536]{1,0:T(8,128)(2,1)S(1)}, bf16[64,1536]{1,0:T(8,128)(2,1)S(1)}, u32[]{:S(2)}, u32[]{:S(2)}) collective-permute-start(bf16[64,1536]{1,0:T(8,128)(2,1)S(1)} %slice.24), channel_id=1, source_target_pairs={{0,128},{128,1},{1,129},{129,2},{2,130},{130,3},{3,131},{131,0},{1... | collective-permute-start | bytes 589832 | tf_op jit(solution)/shard_map/ppermute | solution.py:29
  92.9 6.8 %collective-permute-start.7 = (bf16[64,1536]{1,0:T(8,128)(2,1)S(1)}, bf16[64,1536]{1,0:T(8,128)(2,1)S(1)}, u32[]{:S(2)}, u32[]{:S(2)}) collective-permute-start(bf16[64,1536]{1,0:T(8,128)(2,1)S(1)} %slice.25), channel_id=1, source_target_pairs={{0,131},{128,0},{1,128},{129,1},{2,129},{130,2},{3,130},{131,3},{1... | collective-permute-start | bytes 589832 | tf_op jit(solution)/shard_map/ppermute | solution.py:29
  102.8 16.3 %collective-permute-start.17 = (bf16[1536,384]{1,0:T(8,128)(2,1)S(1)}, bf16[1536,384]{1,0:T(8,128)(2,1)S(1)}, u32[]{:S(2)}, u32[]{:S(2)}) collective-permute-start(bf16[1536,384]{1,0:T(8,128)(2,1)S(1)} %convolution_convert_fusion), channel_id=1, source_target_pairs={{0,4},{128,132},{1,5},{129,133},{2,6},{130,134},{3,7},{131,135},{1... | collective-permute-start | bytes 3538952 | tf_op jit(solution)/shard_map/ppermute | solution.py:29
  106.6 58.1 %collective-permute-start.16 = (bf16[1536,384]{1,0:T(8,128)(2,1)}, bf16[1536,384]{1,0:T(8,128)(2,1)S(1)}, u32[]{:S(2)}, u32[]{:S(2)}) collective-permute-start(bf16[1536,384]{1,0:T(8,128)(2,1)} %convolution_convert_fusion.1), channel_id=1, source_target_pairs={{0,4},{128,132},{1,5},{129,133},{2,6},{130,134},{3,7},{131,135},{1... | collective-permute-start | bytes 3538952 | tf_op jit(solution)/shard_map/ppermute | solution.py:29
  120.4 44.3 %collective-permute-start.18 = (bf16[1536,384]{1,0:T(8,128)(2,1)}, bf16[1536,384]{1,0:T(8,128)(2,1)}, u32[]{:S(2)}, u32[]{:S(2)}) collective-permute-start(bf16[1536,384]{1,0:T(8,128)(2,1)} %add_convert_fusion), channel_id=1, source_target_pairs={{0,12},{128,140},{1,13},{129,141},{2,14},{130,142},{3,15},{131,143... | collective-permute-start | bytes 3538952 | tf_op jit(solution)/shard_map/ppermute | solution.py:29
  120.9 22.5 %collective-permute-start.19 = (f32[1536]{0:T(1024)S(1)}, f32[1536]{0:T(1024)S(1)}, u32[]{:S(2)}, u32[]{:S(2)}) collective-permute-start(f32[1536]{0:T(1024)S(1)} %reduce), channel_id=1, source_target_pairs={{0,4},{128,132},{1,5},{129,133},{2,6},{130,134},{3,7},{131,135},{1... | collective-permute-start | bytes 18440 | tf_op jit(solution)/shard_map/ppermute | solution.py:29
  143.4 4.9 %collective-permute-start.20 = (f32[1536]{0:T(1024)S(1)}, f32[1536]{0:T(1024)S(1)}, u32[]{:S(2)}, u32[]{:S(2)}) collective-permute-start(f32[1536]{0:T(1024)S(1)} %add.38), channel_id=1, source_target_pairs={{0,12},{128,140},{1,13},{129,141},{2,14},{130,142},{3,15},{131,143... | collective-permute-start | bytes 18440 | tf_op jit(solution)/shard_map/ppermute | solution.py:29
  148.3 3.7 %collective-permute-start.21 = (f32[1536]{0:T(1024)S(1)}, f32[1536]{0:T(1024)S(1)}, u32[]{:S(2)}, u32[]{:S(2)}) collective-permute-start(f32[1536]{0:T(1024)S(1)} %add.39), channel_id=1, source_target_pairs={{0,128},{128,0},{1,129},{129,1},{2,130},{130,2},{3,131},{131,3},{1... | collective-permute-start | bytes 18440 | tf_op jit(solution)/shard_map/ppermute | solution.py:29
  151.9 4.5 %collective-permute-start.22 = (f32[1536]{0:T(1024)S(1)}, f32[1536]{0:T(1024)S(1)}, u32[]{:S(2)}, u32[]{:S(2)}) collective-permute-start(f32[1536]{0:T(1024)S(1)} %add.40), channel_id=1, source_target_pairs={{0,1},{128,129},{1,0},{129,128},{2,3},{130,131},{3,2},{131,130},{1... | collective-permute-start | bytes 18440 | tf_op jit(solution)/shard_map/ppermute | solution.py:29
  156.5 7.6 %collective-permute-start.23 = (f32[1536]{0:T(1024)S(1)}, f32[1536]{0:T(1024)S(1)}, u32[]{:S(2)}, u32[]{:S(2)}) collective-permute-start(f32[1536]{0:T(1024)S(1)} %add.41), channel_id=1, source_target_pairs={{0,2},{128,130},{1,3},{129,131},{2,0},{130,128},{3,1},{131,129},{1... | collective-permute-start | bytes 18440 | tf_op jit(solution)/shard_map/ppermute | solution.py:29

commit v3 on v2

--- a/solution.py
+++ b/solution.py
@@ -7,7 +7,6 @@
 
 
 AXES = ("arcs", "trow", "tcol")
-CHUNKS = 1
 VMEM = pl.BlockSpec(memory_space=pltpu.VMEM)
 SMEM = pl.BlockSpec(memory_space=pltpu.SMEM)
 
@@ -37,8 +36,8 @@
     return where
 
 
-def round_y(x, y, core, zh, zl):
-    return x, (y + (1 if core == 0 else 3)) % 4, core, zh, zl
+def along_y(step):
+    return lambda x, y, core, zh, zl: (x, (y + step) % 4, core, zh, zl)
 
 
 def other_core(x, y, core, zh, zl):
@@ -61,18 +60,27 @@
     return where
 
 
-def to_share(turn):
+def across_y(x, y, core, zh, zl):
+    return x, 3 - y, core, zh, zl
+
+
+def handed(core_of_four, sign):
     def where(x, y, core, zh, zl):
-        a = y // 2
-        return x, (y if zl == a else 3 - y), core, (zh + turn) % 4, a
+        z = zh * 2 + zl
+        if y // 2 == zl:
+            z, y = (z + 2 * sign) % 8, 3 - y
+        elif core == core_of_four:
+            z = (z + 3 * sign) % 8
+        else:
+            y = 3 - y
+        return x, y, core, z // 2, z % 2
 
     return where
 
 
 def centre(where_ref, design_ref, small_ref, *refs):
-    chunk_refs, share_refs = refs[:CHUNKS], refs[CHUNKS : CHUNKS + 4]
-    rhs_ref, out_ref = refs[CHUNKS + 4 :]
-    rows, cols = design_ref.shape
+    out_ref, rhs_ref = refs
+    rows, _ = design_ref.shape
     arcs = (small_ref.shape[1] - rows) // 2
     length = rows // arcs
     slot = lax.broadcasted_iota(jnp.int32, (length, 1), 0).astype(jnp.float32)
@@ -101,13 +109,50 @@
     ).astype(jnp.bfloat16)
     sums = jnp.dot(parts, out_ref[...], preferred_element_type=jnp.float32)
     rhs_ref[...] = jnp.sum(sums, axis=0, keepdims=True)
-    narrow = cols // 4
-    for turn, share_ref in enumerate(share_refs):
-        start = pl.multiple_of(((where_ref[3] + turn) % 4) * narrow, 128)
-        share_ref[...] = out_ref[:, pl.ds(start, narrow)]
-    wide = cols // CHUNKS
-    for c, chunk_ref in enumerate(chunk_refs):
-        chunk_ref[...] = out_ref[:, c * wide : (c + 1) * wide]
+
+
+def pick(where_ref, first_ref, second_ref, out_ref):
+    start = pl.multiple_of(where_ref[3] * out_ref.shape[2], 128)
+    out_ref[0] = first_ref[:, pl.ds(start, out_ref.shape[2])]
+    out_ref[1] = second_ref[:, pl.ds(start, out_ref.shape[2])]
+
+
+def pick_for_others(where_ref, ahead_ref, behind_ref, first_ref, second_ref):
+    y, zh, zl = where_ref[1], where_ref[3], where_ref[4]
+    z, wide = 2 * zh + zl, first_ref.shape[1]
+    links = jnp.where(y // 2 == zl, 2, 3)
+    start = (z + 8 - links) % 8 // 2 * wide
+    first_ref[...] = ahead_ref[:, pl.ds(pl.multiple_of(start, 128), wide)]
+    start = (z + links) % 8 // 2 * wide
+    second_ref[...] = behind_ref[:, pl.ds(pl.multiple_of(start, 128), wide)]
+
+
+def make_share(where_ref, behind1_ref, ahead2_ref, behind2_ref, here_ref, first_ref, second_ref, out_ref):
+    y, zh, zl = where_ref[1], where_ref[3], where_ref[4]
+    wide = out_ref.shape[2]
+    start = pl.multiple_of(zh * wide, 128)
+    near = y // 2 == zl
+
+    @pl.when(near)
+    def _():
+        out_ref[0] = behind1_ref[:, pl.ds(start, wide)]
+        out_ref[1] = ahead2_ref[:, pl.ds(start, wide)]
+        out_ref[2] = behind2_ref[:, pl.ds(start, wide)]
+
+    @pl.when(near & (where_ref[2] == 0))
+    def _():
+        out_ref[3] = first_ref[...]
+
+    @pl.when(near & (where_ref[2] == 1))
+    def _():
+        out_ref[3] = second_ref[...]
+
+    @pl.when(jnp.logical_not(near))
+    def _():
+        out_ref[0] = here_ref[0]
+        out_ref[1] = here_ref[1]
+        out_ref[2] = first_ref[...]
+        out_ref[3] = second_ref[...]
 
 
 def joined(columns):
@@ -134,23 +179,27 @@
     )(*flat)
 
 
-def place(where_ref, mine_ref, theirs_ref, cols_out):
-    x, y, core, zh, zl = (where_ref[i] for i in range(5))
-    z = 2 * zh + zl
+def place(where_ref, *refs):
+    refs, cols_out = refs[:-1], refs[-1]
+    x, y, core, _, zl = (where_ref[i] for i in range(5))
     first = jnp.where(core == 0, 1, 3)
-    for other, ref in enumerate((mine_ref, theirs_ref)):
+
+    def put(source_core, offset, turn, ref, row):
+        from_y = (y + offset) % 4
+        near = from_y // 2 == zl
+        of_y = jnp.where(near, from_y, 3 - from_y)
+        m = (2 * (of_y % 2) + source_core) ^ x
+        spot = jnp.where(m == 0, 0, jnp.where(m == 2, 3, jnp.where(m == first, 2, 1)))
+        ahead = jnp.where(near, (7, 2, 6, 4)[turn], (0, 1, 3, 5)[turn])
+        cols_out[spot, pl.ds(pl.multiple_of(ahead * 128, 128), 128), :] = ref[row]
+
+    for other in range(2):
         source_core = (core + other) % 2
-        for step in range(4):
-            from_y = (y + jnp.where(source_core == 0, 4 - step, step)) % 4
-            near = from_y // 2 == zl
-            of_y = jnp.where(near, from_y, 3 - from_y)
-            of_zl = jnp.where(near, zl, 1 - zl)
-            m = (2 * (of_y % 2) + source_core) ^ x
-            spot = jnp.where(m == 0, 0, jnp.where(m == 2, 3, jnp.where(m == first, 2, 1)))
-            for turn in range(4):
-                of_z = 2 * ((zh + 4 - turn) % 4) + of_zl
-                ahead = (of_z + 8 - z) % 8
-                cols_out[spot, pl.ds(pl.multiple_of(ahead * 128, 128), 128), :] = ref[4 * step + turn]
+        near_ref, far_ref = refs[2 * other : 2 * other + 2]
+        for turn in range(4):
+            for step, offset in enumerate((0, 3, 1)):
+                put(source_core, offset, turn, near_ref, 4 * step + turn)
+            put(source_core, 2, turn, far_ref, turn)
 
 
 def product(left, right):
@@ -166,43 +215,52 @@
     where = jnp.stack([tcol // 4, trow // 2, trow % 2, tcol % 4, lax.axis_index("arcs")])
 
     small = jnp.concatenate([observed, arc_weight, arc_counts.astype(f32)])
-    out = pl.pallas_call(
+    centered, rhs = pl.pallas_call(
         centre,
-        out_shape=[jax.ShapeDtypeStruct((rows, cols // CHUNKS), bf16)] * CHUNKS
-        + [jax.ShapeDtypeStruct((rows, narrow), bf16)] * 4
-        + [jax.ShapeDtypeStruct((1, cols), f32)],
+        out_shape=[jax.ShapeDtypeStruct((rows, cols), bf16), jax.ShapeDtypeStruct((1, cols), f32)],
         in_specs=[SMEM, VMEM, VMEM],
-        out_specs=[VMEM] * (CHUNKS + 5),
-        scratch_shapes=[pltpu.VMEM((rows, cols), bf16)],
+        out_specs=[VMEM] * 2,
         compiler_params=pltpu.CompilerParams(vmem_limit_bytes=8 << 20),
         name="centre",
     )(where, design, small.reshape(1, -1))
-    own, shares, rhs = out[:CHUNKS], out[CHUNKS:-1], out[-1].reshape(cols)
-
-    mine = [jnp.concatenate([moved(shares[turn], to_share(turn))[None] for turn in range(4)])]
+    rhs = rhs.reshape(cols)
+
+    up, down = [centered], [centered]
     for _ in range(1, 4):
-        mine.append(moved(mine[-1], round_y))
-    mine = joined([mine])
-    theirs = moved(mine, other_core)
+        up.append(moved(up[-1], along_z(1)))
+        down.append(moved(down[-1], along_z(-1)))
+    half = rows // 2
+    far = [moved(up[3][:half], along_z(1)), moved(down[3][half:], along_z(-1))]
+    left = joined([[centered, *down[1:], *far, up[3], up[2], up[1]]])
+
+    def small_call(kernel, pieces, *shapes):
+        return pl.pallas_call(
+            kernel,
+            out_shape=[jax.ShapeDtypeStruct(shape, bf16) for shape in shapes],
+            in_specs=[SMEM] + [VMEM] * len(pieces),
+            out_specs=[VMEM] * len(shapes),
+            compiler_params=pltpu.CompilerParams(vmem_limit_bytes=8 << 20),
+        )(where, *pieces)
+
+    (here,) = small_call(pick, [centered, down[1]], (2, rows, narrow))
+    here = moved(here, across_y)
+    first, second = small_call(pick_for_others, [down[1], up[1]], (rows, narrow), (rows, narrow))
+    first, second = moved(first, handed(0, -1)), moved(second, handed(1, 1))
+    (share,) = small_call(
+        make_share, [up[1], down[2], up[2], here, first, second], (4, rows, narrow)
+    )
+    y1u, y1d = moved(share, along_y(1)), moved(share, along_y(-1))
+    y2u, y2d = moved(y1u[:2], along_y(1)), moved(y1d[2:], along_y(-1))
+    mine = [joined([[share, y1u, y1d]]), joined([[y2u, y2d]])]
+    theirs = [moved(part, other_core) for part in mine]
     right = pl.pallas_call(
         place,
         out_shape=jax.ShapeDtypeStruct((4, 8 * rows, narrow), bf16),
-        in_specs=[SMEM, VMEM, VMEM],
+        in_specs=[SMEM] + [VMEM] * 4,
         out_specs=VMEM,
         compiler_params=pltpu.CompilerParams(vmem_limit_bytes=12 << 20),
         name="place",
-    )(where, mine, theirs)
-
-    half = rows // 2
-    columns = []
-    for piece in own:
-        up, down = [piece], [piece]
-        for _ in range(1, 4):
-            up.append(moved(up[-1], along_z(1)))
-            down.append(moved(down[-1], along_z(-1)))
-        far = [moved(up[3][:half], along_z(1)), moved(down[3][half:], along_z(-1))]
-        columns.append([piece, *down[1:], *far, up[3], up[2], up[1]])
-    left = joined(columns)
+    )(where, *mine, *theirs)
 
     far = moved(product(left, right[3]).astype(bf16), first_x)
     near = moved(product(left, right[2]).astype(bf16), first_x)

time: 168 us -> 135 us (0.80)
  waiting for transfers between devices: 109 us -> 75.6 us
    ppermute x24 -> x25, waiting for transfers between devices: 109 us -> 75.6 us  [moved(): return lax.ppermute(value, AXES, pairs)]
    pallas_call x1 -> x4, Pallas kernels: 1.04 us -> 2.74 us  [the longest x3 1.75 us: small_call(): pl.pallas_call(kernel, out_shape=[jax.ShapeDtypeStruct(shape, bf16) for s...]
    ppermute x24 -> x25, starting transfers between devices: 39.2 us -> 38.8 us  [moved(): return lax.ppermute(value, AXES, pairs)]
  transfers between devices with their start and end apart: 24 -> 25, of which waited for: 14 -> 16; matrix products, arithmetic and copies ran while one was open for 5% -> 6% of each run, Pallas kernels for 0% -> 1%
where the time goes in v3:
time: 135 us
  waiting for transfers between devices  75.6 us (56%)
  starting transfers between devices  38.8 us (29%)
  matrix products  8.46 us (6%)
  other arithmetic  6.43 us (5%)
  Pallas kernels  3.97 us (3%)
    ppermute x25, waiting for transfers between devices, moved(): return lax.ppermute(value, AXES, pairs)  75.6 us
    ppermute x25, starting transfers between devices, moved(): return lax.ppermute(value, AXES, pairs)  38.8 us
    dot_general x4, matrix products, product(): lax.dot_general(left, right, (((0,), (0,)), ((), ())), preferred_element_...  8.46 us
    mul x1, other arithmetic, local(): gram = (tile + near.astype(f32) + last.astype(f32)) * (1.0 / obs_total)  3.11 us
  transfers between devices with their start and end apart: 25, of which 16 were waited for; matrix products, arithmetic and copies ran while one was open for 6% of the time, Pallas kernels for 1%

profile of v3, /device:TPU:6, one launch (start us, length us, event | category | flops | bytes accessed | tf_op | source)
XLA Modules:
  0.0 135.3 jit_solution(11615108297243379004)
XLA Ops:
  0.7 0.7 convert_element_type.21
  1.3 0.7 pad_maximum_fusion
  2.1 0.1 stack.23.where_ref
  2.2 1.0 copy-done
  3.2 1.0 centre.1
  4.1 5.9 %collective-permute-start = (bf16[128,1536]{1,0:T(8,128)(2,1)S(1)}, bf16[128,1536]{1,0:T(8,128)(2,1)S(1)}, u32[]{:S(2)}, u32[]{:S(2)}) collective-permute-start(bf16[128,1536]{1,0:T(8,128)(2,1)S(1)} %get-tuple-element.8.refs_0_.first_ref), channel_id=1, source_target_pairs={{0,131},{128,0},{1,128},{129,1},{2,129},{130,2},{3,130},{131,3},{1... | collective-permute-start | bytes 1179656 | tf_op jit(solution)/shard_map/ppermute | solution.py:28
  10.1 8.4 %collective-permute-done.refs_1_.second_ref.ahead_ref = bf16[128,1536]{1,0:T(8,128)(2,1)S(1)} collective-permute-done((bf16[128,1536]{1,0:T(8,128)(2,1)S(1)}, bf16[128,1536]{1,0:T(8,128)(2,1)S(1)}, u32[]{:S(2)}, u32[]{:S(2)}) %collective-permute-start) | collective-permute-done | bytes 393248 | tf_op jit(solution)/shard_map/ppermute | solution.py:28
  18.5 3.7 %collective-permute-start.1 = (bf16[128,1536]{1,0:T(8,128)(2,1)S(1)}, bf16[128,1536]{1,0:T(8,128)(2,1)S(1)}, u32[]{:S(2)}, u32[]{:S(2)}) collective-permute-start(bf16[128,1536]{1,0:T(8,128)(2,1)S(1)} %collective-permute-done.refs_1_.second_ref.ahead_ref), channel_id=1, source_target_pairs={{0,131},{128,0},{1,128},{129,1},{2,129},{130,2},{3,130},{131,3},{1... | collective-permute-start | bytes 1179656 | tf_op jit(solution)/shard_map/ppermute | solution.py:28
  22.1 0.0 collective-permute-done.3.refs_8_.behind_ref.behind1_ref
  22.1 0.0 collective-permute-start.4
  22.2 0.6 shard_map.60
  22.7 3.1 %collective-permute-start.8 = (bf16[2,128,384]{2,1,0:T(8,128)(2,1)S(1)}, bf16[2,128,384]{2,1,0:T(8,128)(2,1)S(1)}, u32[]{:S(2)}, u32[]{:S(2)}) collective-permute-start(bf16[2,128,384]{2,1,0:T(8,128)(2,1)S(1)} %shard_map.60), channel_id=1, source_target_pairs={{0,96},{128,224},{1,97},{129,225},{2,98},{130,226},{3,99},{131,227... | collective-permute-start | bytes 589832 | tf_op jit(solution)/shard_map/ppermute | solution.py:28
  25.8 0.6 shard_map.61
  26.4 0.1 collective-permute-start.10
  26.5 4.1 %collective-permute-start.9 = (bf16[128,384]{1,0:T(8,128)(2,1)S(1)}, bf16[128,384]{1,0:T(8,128)(2,1)S(1)}, u32[]{:S(2)}, u32[]{:S(2)}) collective-permute-start(bf16[128,384]{1,0:T(8,128)(2,1)S(1)} %get-tuple-element.9), channel_id=1, source_target_pairs={{0,99},{128,3},{1,96},{129,0},{2,97},{130,1},{3,98},{131,2},{16,11... | collective-permute-start | bytes 294920 | tf_op jit(solution)/shard_map/ppermute | solution.py:28
  30.6 1.7 %collective-permute-done.10.second_ref = bf16[128,384]{1,0:T(8,128)(2,1)S(1)} collective-permute-done((bf16[128,384]{1,0:T(8,128)(2,1)S(1)}, bf16[128,384]{1,0:T(8,128)(2,1)S(1)}, u32[]{:S(2)}, u32[]{:S(2)}) %collective-permute-start.10) | collective-permute-done | bytes 98336 | tf_op jit(solution)/shard_map/ppermute | solution.py:28
  32.3 1.5 %collective-permute-done.9.first_ref = bf16[128,384]{1,0:T(8,128)(2,1)S(1)} collective-permute-done((bf16[128,384]{1,0:T(8,128)(2,1)S(1)}, bf16[128,384]{1,0:T(8,128)(2,1)S(1)}, u32[]{:S(2)}, u32[]{:S(2)}) %collective-permute-start.9) | collective-permute-done | bytes 98336 | tf_op jit(solution)/shard_map/ppermute | solution.py:28
  33.8 3.5 %collective-permute-done.4.refs_7_.behind2_ref = bf16[128,1536]{1,0:T(8,128)(2,1)S(1)} collective-permute-done((bf16[128,1536]{1,0:T(8,128)(2,1)S(1)}, bf16[128,1536]{1,0:T(8,128)(2,1)S(1)}, u32[]{:S(2)}, u32[]{:S(2)}) %collective-permute-start.4) | collective-permute-done | bytes 393248 | tf_op jit(solution)/shard_map/ppermute | solution.py:28
  37.3 0.6 shard_map.62.refs_0_
  37.9 1.7 %collective-permute-start.11 = (bf16[4,128,384]{2,1,0:T(8,128)(2,1)S(1)}, bf16[4,128,384]{2,1,0:T(8,128)(2,1)S(1)}, u32[]{:S(2)}, u32[]{:S(2)}) collective-permute-start(bf16[4,128,384]{2,1,0:T(8,128)(2,1)S(1)} %shard_map.62.refs_0_), channel_id=1, source_target_pairs={{0,32},{128,160},{1,33},{129,161},{2,34},{130,162},{3,35},{131,163... | collective-permute-start | bytes 1179656 | tf_op jit(solution)/shard_map/ppermute | solution.py:28
  39.6 1.7 %collective-permute-start.12 = (bf16[4,128,384]{2,1,0:T(8,128)(2,1)S(1)}, bf16[4,128,384]{2,1,0:T(8,128)(2,1)S(1)}, u32[]{:S(2)}, u32[]{:S(2)}) collective-permute-start(bf16[4,128,384]{2,1,0:T(8,128)(2,1)S(1)} %shard_map.62.refs_0_), channel_id=1, source_target_pairs={{0,96},{128,224},{1,97},{129,225},{2,98},{130,226},{3,99},{131,227... | collective-permute-start | bytes 1179656 | tf_op jit(solution)/shard_map/ppermute | solution.py:28
  41.2 5.9 %collective-permute-done.11.refs_1_ = bf16[4,128,384]{2,1,0:T(8,128)(2,1)S(1)} collective-permute-done((bf16[4,128,384]{2,1,0:T(8,128)(2,1)S(1)}, bf16[4,128,384]{2,1,0:T(8,128)(2,1)S(1)}, u32[]{:S(2)}, u32[]{:S(2)}) %collective-permute-start.11) | collective-permute-done | bytes 393248 | tf_op jit(solution)/shard_map/ppermute | solution.py:28
  47.1 0.2 collective-permute-done.12.refs_2_
  47.3 0.1 shard_map.63.refs_0_
  47.4 0.1 collective-permute-start.15
  47.5 3.3 %collective-permute-start.5 = (bf16[128,1536]{1,0:T(8,128)(2,1)S(1)}, bf16[128,1536]{1,0:T(8,128)(2,1)S(1)}, u32[]{:S(2)}, u32[]{:S(2)}) collective-permute-start(bf16[128,1536]{1,0:T(8,128)(2,1)S(1)} %collective-permute-done.4.refs_7_.behind2_ref), channel_id=1, source_target_pairs={{0,128},{128,1},{1,129},{129,2},{2,130},{130,3},{3,131},{131,0},{1... | collective-permute-start | bytes 1179656 | tf_op jit(solution)/shard_map/ppermute | solution.py:28
  50.9 0.0 collective-permute-start.2
  50.9 0.3 collective-permute-start.13
  51.2 3.1 %collective-permute-start.14 = (bf16[2,128,384]{2,1,0:T(8,128)(2,1)S(1)}, bf16[2,128,384]{2,1,0:T(8,128)(2,1)S(1)}, u32[]{:S(2)}, u32[]{:S(2)}) collective-permute-start(bf16[2,128,384]{2,1,0:T(8,128)(2,1)S(1)} %slice.35), channel_id=1, source_target_pairs={{0,96},{128,224},{1,97},{129,225},{2,98},{130,226},{3,99},{131,227... | collective-permute-start | bytes 589832 | tf_op jit(solution)/shard_map/ppermute | solution.py:28
  54.3 4.8 %collective-permute-done.13.refs_0_ = bf16[2,128,384]{2,1,0:T(8,128)(2,1)S(1)} collective-permute-done((bf16[2,128,384]{2,1,0:T(8,128)(2,1)S(1)}, bf16[2,128,384]{2,1,0:T(8,128)(2,1)S(1)}, u32[]{:S(2)}, u32[]{:S(2)}) %collective-permute-start.13) | collective-permute-done | bytes 196640 | tf_op jit(solution)/shard_map/ppermute | solution.py:28
  59.1 0.0 collective-permute-done.14.refs_1_
  59.2 0.1 collective-permute-start.16
  59.3 1.0 collective-permute-done.5.refs_6_
  60.3 2.3 %collective-permute-start.6 = (bf16[64,1536]{1,0:T(8,128)(2,1)S(1)}, bf16[64,1536]{1,0:T(8,128)(2,1)S(1)}, u32[]{:S(2)}, u32[]{:S(2)}) collective-permute-start(bf16[64,1536]{1,0:T(8,128)(2,1)S(1)} %slice.32), channel_id=1, source_target_pairs={{0,128},{128,1},{1,129},{129,2},{2,130},{130,3},{3,131},{131,0},{1... | collective-permute-start | bytes 589832 | tf_op jit(solution)/shard_map/ppermute | solution.py:28
  62.6 1.3 collective-permute-start.7
  63.9 4.2 %collective-permute-done.6.refs_4_ = bf16[64,1536]{1,0:T(8,128)(2,1)S(1)} collective-permute-done((bf16[64,1536]{1,0:T(8,128)(2,1)S(1)}, bf16[64,1536]{1,0:T(8,128)(2,1)S(1)}, u32[]{:S(2)}, u32[]{:S(2)}) %collective-permute-start.6) | collective-permute-done | bytes 196640 | tf_op jit(solution)/shard_map/ppermute | solution.py:28
  68.1 0.6 collective-permute-done.7.refs_5_
  68.8 0.2 shard_map.59
  69.0 0.0 collective-permute-done.16.refs_3_
  69.0 0.0 collective-permute-done.15.refs_2_
  69.0 0.9 place.1
  69.9 1.9 %convolution_convert_fusion = bf16[1536,384]{1,0:T(8,128)(2,1)S(1)} fusion(bf16[1024,1536]{1,0:T(8,128)(2,1)S(1)} %shard_map.59, bf16[4,1024,384]{2,1,0:T(8,128)(2,1)S(1)} %place.1), kind=kOutput, calls=%fused_computation | convolution fusion | flops 1208549376 | bytes 5111808 | tf_op jit(solution)/shard_map/dot_general | solution.py:206
  71.8 0.9 collective-permute-start.18
  72.7 1.9 %fusion = f32[1536,384]{1,0:T(8,128)S(1)} fusion(bf16[1024,1536]{1,0:T(8,128)(2,1)S(1)} %shard_map.59, bf16[4,1024,384]{2,1,0:T(8,128)(2,1)S(1)} %place.1), kind=kOutput, calls=%fused_computation.7 | convolution fusion | flops 1207959552 | bytes 6291456 | tf_op jit(solution)/shard_map/dot_general | solution.py:206
  74.5 1.9 %fusion.1 = f32[1536,384]{1,0:T(8,128)S(1)} fusion(bf16[1024,1536]{1,0:T(8,128)(2,1)S(1)} %shard_map.59, bf16[4,1024,384]{2,1,0:T(8,128)(2,1)S(1)} %place.1), kind=kOutput, calls=%fused_computation.9 | convolution fusion | flops 1207959552 | bytes 6291456 | tf_op jit(solution)/shard_map/dot_general | solution.py:206
  76.4 2.9 %convolution_convert_fusion.1 = bf16[1536,384]{1,0:T(8,128)(2,1)} fusion(bf16[1024,1536]{1,0:T(8,128)(2,1)S(1)} %shard_map.59, bf16[4,1024,384]{2,1,0:T(8,128)(2,1)S(1)} %place.1), kind=kOutput, calls=%fused_computation.1 | convolution fusion | flops 1208549376 | bytes 5111808 | tf_op jit(solution)/shard_map/dot_general | solution.py:206
  79.3 1.2 collective-permute-start.17
  80.5 7.6 %collective-permute-done.18 = bf16[1536,384]{1,0:T(8,128)(2,1)S(1)} collective-permute-done((bf16[1536,384]{1,0:T(8,128)(2,1)S(1)}, bf16[1536,384]{1,0:T(8,128)(2,1)S(1)}, u32[]{:S(2)}, u32[]{:S(2)}) %collective-permute-start.18) | collective-permute-done | bytes 1179680 | tf_op jit(solution)/shard_map/ppermute | solution.py:28
  88.0 1.3 add_convert_fusion
  89.3 0.5 collective-permute-start.19
  89.8 1.0 collective-permute-start.20
  90.8 20.1 %collective-permute-done.20 = f32[1536]{0:T(1024)S(1)} collective-permute-done((f32[1536]{0:T(1024)S(1)}, f32[1536]{0:T(1024)S(1)}, u32[]{:S(2)}, u32[]{:S(2)}) %collective-permute-start.20) | collective-permute-done | bytes 6176 | tf_op jit(solution)/shard_map/ppermute | solution.py:28
  110.9 0.5 collective-permute-start.21
  111.4 4.4 %collective-permute-done.21 = f32[1536]{0:T(1024)S(1)} collective-permute-done((f32[1536]{0:T(1024)S(1)}, f32[1536]{0:T(1024)S(1)}, u32[]{:S(2)}, u32[]{:S(2)}) %collective-permute-start.21) | collective-permute-done | bytes 6176 | tf_op jit(solution)/shard_map/ppermute | solution.py:28
  115.8 1.5 %collective-permute-start.22 = (f32[1536]{0:T(1024)S(1)}, f32[1536]{0:T(1024)S(1)}, u32[]{:S(2)}, u32[]{:S(2)}) collective-permute-start(f32[1536]{0:T(1024)S(1)} %add.39), channel_id=1, source_target_pairs={{0,128},{128,0},{1,129},{129,1},{2,130},{130,2},{3,131},{131,3},{1... | collective-permute-start | bytes 18440 | tf_op jit(solution)/shard_map/ppermute | solution.py:28
  117.3 2.2 %collective-permute-done.22 = f32[1536]{0:T(1024)S(1)} collective-permute-done((f32[1536]{0:T(1024)S(1)}, f32[1536]{0:T(1024)S(1)}, u32[]{:S(2)}, u32[]{:S(2)}) %collective-permute-start.22) | collective-permute-done | bytes 6176 | tf_op jit(solution)/shard_map/ppermute | solution.py:28
  119.5 1.2 collective-permute-start.23
  120.7 3.4 %collective-permute-done.23 = f32[1536]{0:T(1024)S(1)} collective-permute-done((f32[1536]{0:T(1024)S(1)}, f32[1536]{0:T(1024)S(1)}, u32[]{:S(2)}, u32[]{:S(2)}) %collective-permute-start.23) | collective-permute-done | bytes 6176 | tf_op jit(solution)/shard_map/ppermute | solution.py:28
  124.0 1.4 %collective-permute-start.24 = (f32[1536]{0:T(1024)S(1)}, f32[1536]{0:T(1024)S(1)}, u32[]{:S(2)}, u32[]{:S(2)}) collective-permute-start(f32[1536]{0:T(1024)S(1)} %add.41), channel_id=1, source_target_pairs={{0,2},{128,130},{1,3},{129,131},{2,0},{130,128},{3,1},{131,129},{1... | collective-permute-start | bytes 18440 | tf_op jit(solution)/shard_map/ppermute | solution.py:28
  125.4 6.1 %collective-permute-done.24 = f32[1536]{0:T(1024)S(1)} collective-permute-done((f32[1536]{0:T(1024)S(1)}, f32[1536]{0:T(1024)S(1)}, u32[]{:S(2)}, u32[]{:S(2)}) %collective-permute-start.24) | collective-permute-done | bytes 6176 | tf_op jit(solution)/shard_map/ppermute | solution.py:28
  131.6 0.6 add_multiply_fusion.1
  132.2 0.0 collective-permute-done.17
  132.2 0.0 collective-permute-done.19
  132.2 3.1 %add_multiply_fusion = f32[1536,384]{1,0:T(8,128)} fusion(bf16[1536,384]{1,0:T(8,128)(2,1)} %collective-permute-done.19, f32[1536,384]{1,0:T(8,128)S(1)} %fusion, bf16[1536,384]{1,0:T(8,128)(2,1)S(1)} %collective-permute-done.17), kind=kLoop, calls=%fused_computation.2 | loop fusion | flops 2949120 | bytes 7077888 | tf_op jit(solution)/shard_map/mul | solution.py:269
  (15 shorter events, 0.1 us)
Async XLA Ops:
  2.2 1.0 copy-start
  4.1 14.3 %collective-permute-start = (bf16[128,1536]{1,0:T(8,128)(2,1)S(1)}, bf16[128,1536]{1,0:T(8,128)(2,1)S(1)}, u32[]{:S(2)}, u32[]{:S(2)}) collective-permute-start(bf16[128,1536]{1,0:T(8,128)(2,1)S(1)} %get-tuple-element.8.refs_0_.first_ref), channel_id=1, source_target_pairs={{0,131},{128,0},{1,128},{129,1},{2,129},{130,2},{3,130},{131,3},{1... | collective-permute-start | bytes 1179656 | tf_op jit(solution)/shard_map/ppermute | solution.py:28
  10.1 12.1 %collective-permute-start.3 = (bf16[128,1536]{1,0:T(8,128)(2,1)S(1)}, bf16[128,1536]{1,0:T(8,128)(2,1)S(1)}, u32[]{:S(2)}, u32[]{:S(2)}) collective-permute-start(bf16[128,1536]{1,0:T(8,128)(2,1)S(1)} %get-tuple-element.8.refs_0_.first_ref), channel_id=1, source_target_pairs={{0,128},{128,1},{1,129},{129,2},{2,130},{130,3},{3,131},{131,0},{1... | collective-permute-start | bytes 1179656 | tf_op jit(solution)/shard_map/ppermute | solution.py:28
  18.5 15.4 %collective-permute-start.1 = (bf16[128,1536]{1,0:T(8,128)(2,1)S(1)}, bf16[128,1536]{1,0:T(8,128)(2,1)S(1)}, u32[]{:S(2)}, u32[]{:S(2)}) collective-permute-start(bf16[128,1536]{1,0:T(8,128)(2,1)S(1)} %collective-permute-done.refs_1_.second_ref.ahead_ref), channel_id=1, source_target_pairs={{0,131},{128,0},{1,128},{129,1},{2,129},{130,2},{3,130},{131,3},{1... | collective-permute-start | bytes 1179656 | tf_op jit(solution)/shard_map/ppermute | solution.py:28
  22.1 15.1 %collective-permute-start.4 = (bf16[128,1536]{1,0:T(8,128)(2,1)S(1)}, bf16[128,1536]{1,0:T(8,128)(2,1)S(1)}, u32[]{:S(2)}, u32[]{:S(2)}) collective-permute-start(bf16[128,1536]{1,0:T(8,128)(2,1)S(1)} %collective-permute-done.3.refs_8_.behind_ref.behind1_ref), channel_id=1, source_target_pairs={{0,128},{128,1},{1,129},{129,2},{2,130},{130,3},{3,131},{131,0},{1... | collective-permute-start | bytes 1179656 | tf_op jit(solution)/shard_map/ppermute | solution.py:28
  22.7 11.1 %collective-permute-start.8 = (bf16[2,128,384]{2,1,0:T(8,128)(2,1)S(1)}, bf16[2,128,384]{2,1,0:T(8,128)(2,1)S(1)}, u32[]{:S(2)}, u32[]{:S(2)}) collective-permute-start(bf16[2,128,384]{2,1,0:T(8,128)(2,1)S(1)} %shard_map.60), channel_id=1, source_target_pairs={{0,96},{128,224},{1,97},{129,225},{2,98},{130,226},{3,99},{131,227... | collective-permute-start | bytes 589832 | tf_op jit(solution)/shard_map/ppermute | solution.py:28
  26.4 5.9 %collective-permute-start.10 = (bf16[128,384]{1,0:T(8,128)(2,1)S(1)}, bf16[128,384]{1,0:T(8,128)(2,1)S(1)}, u32[]{:S(2)}, u32[]{:S(2)}) collective-permute-start(bf16[128,384]{1,0:T(8,128)(2,1)S(1)} %get-tuple-element.10), channel_id=1, source_target_pairs={{0,97},{128,224},{1,98},{129,225},{2,99},{130,226},{3,96},{131,227... | collective-permute-start | bytes 294920 | tf_op jit(solution)/shard_map/ppermute | solution.py:28
  26.5 7.3 %collective-permute-start.9 = (bf16[128,384]{1,0:T(8,128)(2,1)S(1)}, bf16[128,384]{1,0:T(8,128)(2,1)S(1)}, u32[]{:S(2)}, u32[]{:S(2)}) collective-permute-start(bf16[128,384]{1,0:T(8,128)(2,1)S(1)} %get-tuple-element.9), channel_id=1, source_target_pairs={{0,99},{128,3},{1,96},{129,0},{2,97},{130,1},{3,98},{131,2},{16,11... | collective-permute-start | bytes 294920 | tf_op jit(solution)/shard_map/ppermute | solution.py:28
  37.9 9.2 %collective-permute-start.11 = (bf16[4,128,384]{2,1,0:T(8,128)(2,1)S(1)}, bf16[4,128,384]{2,1,0:T(8,128)(2,1)S(1)}, u32[]{:S(2)}, u32[]{:S(2)}) collective-permute-start(bf16[4,128,384]{2,1,0:T(8,128)(2,1)S(1)} %shard_map.62.refs_0_), channel_id=1, source_target_pairs={{0,32},{128,160},{1,33},{129,161},{2,34},{130,162},{3,35},{131,163... | collective-permute-start | bytes 1179656 | tf_op jit(solution)/shard_map/ppermute | solution.py:28
  39.6 7.8 %collective-permute-start.12 = (bf16[4,128,384]{2,1,0:T(8,128)(2,1)S(1)}, bf16[4,128,384]{2,1,0:T(8,128)(2,1)S(1)}, u32[]{:S(2)}, u32[]{:S(2)}) collective-permute-start(bf16[4,128,384]{2,1,0:T(8,128)(2,1)S(1)} %shard_map.62.refs_0_), channel_id=1, source_target_pairs={{0,96},{128,224},{1,97},{129,225},{2,98},{130,226},{3,99},{131,227... | collective-permute-start | bytes 1179656 | tf_op jit(solution)/shard_map/ppermute | solution.py:28
  47.4 21.5 %collective-permute-start.15 = (bf16[12,128,384]{2,1,0:T(8,128)(2,1)S(1)}, bf16[12,128,384]{2,1,0:T(8,128)(2,1)S(1)}, u32[]{:S(2)}, u32[]{:S(2)}) collective-permute-start(bf16[12,128,384]{2,1,0:T(8,128)(2,1)S(1)} %shard_map.63.refs_0_), channel_id=1, source_target_pairs={{0,16},{128,144},{1,17},{129,145},{2,18},{130,146},{3,19},{131,147... | collective-permute-start | bytes 3538952 | tf_op jit(solution)/shard_map/ppermute | solution.py:28
  47.5 12.7 %collective-permute-start.5 = (bf16[128,1536]{1,0:T(8,128)(2,1)S(1)}, bf16[128,1536]{1,0:T(8,128)(2,1)S(1)}, u32[]{:S(2)}, u32[]{:S(2)}) collective-permute-start(bf16[128,1536]{1,0:T(8,128)(2,1)S(1)} %collective-permute-done.4.refs_7_.behind2_ref), channel_id=1, source_target_pairs={{0,128},{128,1},{1,129},{129,2},{2,130},{130,3},{3,131},{131,0},{1... | collective-permute-start | bytes 1179656 | tf_op jit(solution)/shard_map/ppermute | solution.py:28
  50.9 11.7 %collective-permute-start.2 = (bf16[128,1536]{1,0:T(8,128)(2,1)S(1)}, bf16[128,1536]{1,0:T(8,128)(2,1)S(1)}, u32[]{:S(2)}, u32[]{:S(2)}) collective-permute-start(bf16[128,1536]{1,0:T(8,128)(2,1)S(1)} %collective-permute-done.1.refs_2_.ahead2_ref), channel_id=1, source_target_pairs={{0,131},{128,0},{1,128},{129,1},{2,129},{130,2},{3,130},{131,3},{1... | collective-permute-start | bytes 1179656 | tf_op jit(solution)/shard_map/ppermute | solution.py:28
  50.9 8.2 %collective-permute-start.13 = (bf16[2,128,384]{2,1,0:T(8,128)(2,1)S(1)}, bf16[2,128,384]{2,1,0:T(8,128)(2,1)S(1)}, u32[]{:S(2)}, u32[]{:S(2)}) collective-permute-start(bf16[2,128,384]{2,1,0:T(8,128)(2,1)S(1)} %slice.34), channel_id=1, source_target_pairs={{0,32},{128,160},{1,33},{129,161},{2,34},{130,162},{3,35},{131,163... | collective-permute-start | bytes 589832 | tf_op jit(solution)/shard_map/ppermute | solution.py:28
  51.2 8.0 %collective-permute-start.14 = (bf16[2,128,384]{2,1,0:T(8,128)(2,1)S(1)}, bf16[2,128,384]{2,1,0:T(8,128)(2,1)S(1)}, u32[]{:S(2)}, u32[]{:S(2)}) collective-permute-start(bf16[2,128,384]{2,1,0:T(8,128)(2,1)S(1)} %slice.35), channel_id=1, source_target_pairs={{0,96},{128,224},{1,97},{129,225},{2,98},{130,226},{3,99},{131,227... | collective-permute-start | bytes 589832 | tf_op jit(solution)/shard_map/ppermute | solution.py:28
  59.2 9.8 %collective-permute-start.16 = (bf16[4,128,384]{2,1,0:T(8,128)(2,1)S(1)}, bf16[4,128,384]{2,1,0:T(8,128)(2,1)S(1)}, u32[]{:S(2)}, u32[]{:S(2)}) collective-permute-start(bf16[4,128,384]{2,1,0:T(8,128)(2,1)S(1)} %shard_map.64.refs_1_), channel_id=1, source_target_pairs={{0,16},{128,144},{1,17},{129,145},{2,18},{130,146},{3,19},{131,147... | collective-permute-start | bytes 1179656 | tf_op jit(solution)/shard_map/ppermute | solution.py:28
  60.3 7.8 %collective-permute-start.6 = (bf16[64,1536]{1,0:T(8,128)(2,1)S(1)}, bf16[64,1536]{1,0:T(8,128)(2,1)S(1)}, u32[]{:S(2)}, u32[]{:S(2)}) collective-permute-start(bf16[64,1536]{1,0:T(8,128)(2,1)S(1)} %slice.32), channel_id=1, source_target_pairs={{0,128},{128,1},{1,129},{129,2},{2,130},{130,3},{3,131},{131,0},{1... | collective-permute-start | bytes 589832 | tf_op jit(solution)/shard_map/ppermute | solution.py:28
  62.6 6.2 %collective-permute-start.7 = (bf16[64,1536]{1,0:T(8,128)(2,1)S(1)}, bf16[64,1536]{1,0:T(8,128)(2,1)S(1)}, u32[]{:S(2)}, u32[]{:S(2)}) collective-permute-start(bf16[64,1536]{1,0:T(8,128)(2,1)S(1)} %slice.33), channel_id=1, source_target_pairs={{0,131},{128,0},{1,128},{129,1},{2,129},{130,2},{3,130},{131,3},{1... | collective-permute-start | bytes 589832 | tf_op jit(solution)/shard_map/ppermute | solution.py:28
  71.8 16.3 %collective-permute-start.18 = (bf16[1536,384]{1,0:T(8,128)(2,1)S(1)}, bf16[1536,384]{1,0:T(8,128)(2,1)S(1)}, u32[]{:S(2)}, u32[]{:S(2)}) collective-permute-start(bf16[1536,384]{1,0:T(8,128)(2,1)S(1)} %convolution_convert_fusion), channel_id=1, source_target_pairs={{0,4},{128,132},{1,5},{129,133},{2,6},{130,134},{3,7},{131,135},{1... | collective-permute-start | bytes 3538952 | tf_op jit(solution)/shard_map/ppermute | solution.py:28
  79.3 52.9 %collective-permute-start.17 = (bf16[1536,384]{1,0:T(8,128)(2,1)}, bf16[1536,384]{1,0:T(8,128)(2,1)S(1)}, u32[]{:S(2)}, u32[]{:S(2)}) collective-permute-start(bf16[1536,384]{1,0:T(8,128)(2,1)} %convolution_convert_fusion.1), channel_id=1, source_target_pairs={{0,4},{128,132},{1,5},{129,133},{2,6},{130,134},{3,7},{131,135},{1... | collective-permute-start | bytes 3538952 | tf_op jit(solution)/shard_map/ppermute | solution.py:28
  89.3 42.9 %collective-permute-start.19 = (bf16[1536,384]{1,0:T(8,128)(2,1)}, bf16[1536,384]{1,0:T(8,128)(2,1)}, u32[]{:S(2)}, u32[]{:S(2)}) collective-permute-start(bf16[1536,384]{1,0:T(8,128)(2,1)} %add_convert_fusion), channel_id=1, source_target_pairs={{0,12},{128,140},{1,13},{129,141},{2,14},{130,142},{3,15},{131,143... | collective-permute-start | bytes 3538952 | tf_op jit(solution)/shard_map/ppermute | solution.py:28
  89.8 21.1 %collective-permute-start.20 = (f32[1536]{0:T(1024)S(1)}, f32[1536]{0:T(1024)S(1)}, u32[]{:S(2)}, u32[]{:S(2)}) collective-permute-start(f32[1536]{0:T(1024)S(1)} %reduce), channel_id=1, source_target_pairs={{0,4},{128,132},{1,5},{129,133},{2,6},{130,134},{3,7},{131,135},{1... | collective-permute-start | bytes 18440 | tf_op jit(solution)/shard_map/ppermute | solution.py:28
  110.9 4.9 %collective-permute-start.21 = (f32[1536]{0:T(1024)S(1)}, f32[1536]{0:T(1024)S(1)}, u32[]{:S(2)}, u32[]{:S(2)}) collective-permute-start(f32[1536]{0:T(1024)S(1)} %add.38), channel_id=1, source_target_pairs={{0,12},{128,140},{1,13},{129,141},{2,14},{130,142},{3,15},{131,143... | collective-permute-start | bytes 18440 | tf_op jit(solution)/shard_map/ppermute | solution.py:28
  115.8 3.7 %collective-permute-start.22 = (f32[1536]{0:T(1024)S(1)}, f32[1536]{0:T(1024)S(1)}, u32[]{:S(2)}, u32[]{:S(2)}) collective-permute-start(f32[1536]{0:T(1024)S(1)} %add.39), channel_id=1, source_target_pairs={{0,128},{128,0},{1,129},{129,1},{2,130},{130,2},{3,131},{131,3},{1... | collective-permute-start | bytes 18440 | tf_op jit(solution)/shard_map/ppermute | solution.py:28
  119.5 4.5 %collective-permute-start.23 = (f32[1536]{0:T(1024)S(1)}, f32[1536]{0:T(1024)S(1)}, u32[]{:S(2)}, u32[]{:S(2)}) collective-permute-start(f32[1536]{0:T(1024)S(1)} %add.40), channel_id=1, source_target_pairs={{0,1},{128,129},{1,0},{129,128},{2,3},{130,131},{3,2},{131,130},{1... | collective-permute-start | bytes 18440 | tf_op jit(solution)/shard_map/ppermute | solution.py:28
  124.0 7.6 %collective-permute-start.24 = (f32[1536]{0:T(1024)S(1)}, f32[1536]{0:T(1024)S(1)}, u32[]{:S(2)}, u32[]{:S(2)}) collective-permute-start(f32[1536]{0:T(1024)S(1)} %add.41), channel_id=1, source_target_pairs={{0,2},{128,130},{1,3},{129,131},{2,0},{130,128},{3,1},{131,129},{1... | collective-permute-start | bytes 18440 | tf_op jit(solution)/shard_map/ppermute | solution.py:28

commit v4 on v3

--- a/solution.py
+++ b/solution.py
@@ -1,3 +1,5 @@
+from functools import partial
+
 import jax
 import jax.numpy as jnp
 from jax import lax
@@ -179,8 +181,8 @@
     )(*flat)
 
 
-def place(where_ref, *refs):
-    refs, cols_out = refs[:-1], refs[-1]
+def place(parts, where_ref, *refs):
+    cols_out = refs[-1]
     x, y, core, _, zl = (where_ref[i] for i in range(5))
     first = jnp.where(core == 0, 1, 3)
 
@@ -193,13 +195,10 @@
         ahead = jnp.where(near, (7, 2, 6, 4)[turn], (0, 1, 3, 5)[turn])
         cols_out[spot, pl.ds(pl.multiple_of(ahead * 128, 128), 128), :] = ref[row]
 
-    for other in range(2):
-        source_core = (core + other) % 2
-        near_ref, far_ref = refs[2 * other : 2 * other + 2]
-        for turn in range(4):
-            for step, offset in enumerate((0, 3, 1)):
-                put(source_core, offset, turn, near_ref, 4 * step + turn)
-            put(source_core, 2, turn, far_ref, turn)
+    for (other, offsets), ref in zip(parts, refs):
+        for step, offset in enumerate(offsets):
+            for turn in range(4):
+                put((core + other) % 2, offset, turn, ref, 4 * step + turn)
 
 
 def product(left, right):
@@ -214,7 +213,12 @@
     trow, tcol = lax.axis_index("trow"), lax.axis_index("tcol")
     where = jnp.stack([tcol // 4, trow // 2, trow % 2, tcol % 4, lax.axis_index("arcs")])
 
-    small = jnp.concatenate([observed, arc_weight, arc_counts.astype(f32)])
+    arcs = arc_counts.shape[0]
+    small = (
+        jnp.pad(observed, (0, 2 * arcs))
+        + jnp.pad(arc_weight, (rows, arcs))
+        + jnp.pad(arc_counts.astype(f32), (rows + arcs, 0))
+    )
     centered, rhs = pl.pallas_call(
         centre,
         out_shape=[jax.ShapeDtypeStruct((rows, cols), bf16), jax.ShapeDtypeStruct((1, cols), f32)],
@@ -253,20 +257,27 @@
     y2u, y2d = moved(y1u[:2], along_y(1)), moved(y1d[2:], along_y(-1))
     mine = [joined([[share, y1u, y1d]]), joined([[y2u, y2d]])]
     theirs = [moved(part, other_core) for part in mine]
-    right = pl.pallas_call(
-        place,
-        out_shape=jax.ShapeDtypeStruct((4, 8 * rows, narrow), bf16),
-        in_specs=[SMEM] + [VMEM] * 4,
-        out_specs=VMEM,
-        compiler_params=pltpu.CompilerParams(vmem_limit_bytes=12 << 20),
-        name="place",
-    )(where, *mine, *theirs)
+
+    def placed(parts, pieces, before=()):
+        return pl.pallas_call(
+            partial(place, parts),
+            out_shape=jax.ShapeDtypeStruct((4, 8 * rows, narrow), bf16),
+            in_specs=[SMEM] + [VMEM] * (len(pieces) + len(before)),
+            out_specs=VMEM,
+            input_output_aliases={1 + len(pieces): 0} if before else {},
+            compiler_params=pltpu.CompilerParams(vmem_limit_bytes=12 << 20),
+        )(where, *pieces, *before)
+
+    close, across = (0, 3, 1), (2,)
+    right = placed(((0, close), (0, across), (1, close)), (*mine, theirs[0]))
+    right = placed(((1, across),), theirs[1:], (right,))
 
     far = moved(product(left, right[3]).astype(bf16), first_x)
     near = moved(product(left, right[2]).astype(bf16), first_x)
     second, tile = lax.optimization_barrier((product(left, right[1]), product(left, right[0])))
     last = moved((second + far.astype(f32)).astype(bf16), second_x)
-    gram = (tile + near.astype(f32) + last.astype(f32)) * (1.0 / obs_total)
+    tile = lax.optimization_barrier(tile + near.astype(f32))
+    gram = (tile + last.astype(f32)) * (1.0 / obs_total)
 
     rhs = rhs + moved(rhs, first_x)
     rhs = rhs + moved(rhs, second_x)

time: 135 us -> 136 us (level)
  transfers between devices with their start and end apart: 25 -> 25, of which waited for: 16 -> 16; matrix products, arithmetic and copies ran while one was open for 6% -> 6% of each run, Pallas kernels for 1% -> 2%
where the time goes in v4:
time: 136 us
  waiting for transfers between devices  75.6 us (56%)
  starting transfers between devices  38.9 us (29%)
  matrix products  8.39 us (6%)
  other arithmetic  6.51 us (5%)
  Pallas kernels  4.54 us (3%)
    ppermute x25, waiting for transfers between devices, moved(): return lax.ppermute(value, AXES, pairs)  75.6 us
    ppermute x25, starting transfers between devices, moved(): return lax.ppermute(value, AXES, pairs)  38.9 us
    dot_general x4, matrix products, product(): lax.dot_general(left, right, (((0,), (0,)), ((), ())), preferred_element_...  8.39 us
    mul x1, other arithmetic, local(): gram = (tile + last.astype(f32)) * (1.0 / obs_total)  2.96 us
  transfers between devices with their start and end apart: 25, of which 16 were waited for; matrix products, arithmetic and copies ran while one was open for 6% of the time, Pallas kernels for 2%

profile of v4, /device:TPU:6, one launch (start us, length us, event | category | flops | bytes accessed | tf_op | source)
XLA Modules:
  0.0 135.9 jit_solution(4368733397389055694)
XLA Ops:
  0.7 0.7 convert_element_type.27
  1.3 0.7 pad_add_fusion
  2.1 0.1 stack.23.where_ref
  2.2 1.0 copy-done
  3.2 1.0 centre.1
  4.1 5.9 %collective-permute-start = (bf16[128,1536]{1,0:T(8,128)(2,1)S(1)}, bf16[128,1536]{1,0:T(8,128)(2,1)S(1)}, u32[]{:S(2)}, u32[]{:S(2)}) collective-permute-start(bf16[128,1536]{1,0:T(8,128)(2,1)S(1)} %get-tuple-element.8.refs_0_.first_ref), channel_id=1, source_target_pairs={{0,131},{128,0},{1,128},{129,1},{2,129},{130,2},{3,130},{131,3},{1... | collective-permute-start | bytes 1179656 | tf_op jit(solution)/shard_map/ppermute | solution.py:30
  10.1 8.4 %collective-permute-done.refs_1_.second_ref.ahead_ref = bf16[128,1536]{1,0:T(8,128)(2,1)S(1)} collective-permute-done((bf16[128,1536]{1,0:T(8,128)(2,1)S(1)}, bf16[128,1536]{1,0:T(8,128)(2,1)S(1)}, u32[]{:S(2)}, u32[]{:S(2)}) %collective-permute-start) | collective-permute-done | bytes 393248 | tf_op jit(solution)/shard_map/ppermute | solution.py:30
  18.5 3.7 %collective-permute-start.1 = (bf16[128,1536]{1,0:T(8,128)(2,1)S(1)}, bf16[128,1536]{1,0:T(8,128)(2,1)S(1)}, u32[]{:S(2)}, u32[]{:S(2)}) collective-permute-start(bf16[128,1536]{1,0:T(8,128)(2,1)S(1)} %collective-permute-done.refs_1_.second_ref.ahead_ref), channel_id=1, source_target_pairs={{0,131},{128,0},{1,128},{129,1},{2,129},{130,2},{3,130},{131,3},{1... | collective-permute-start | bytes 1179656 | tf_op jit(solution)/shard_map/ppermute | solution.py:30
  22.1 0.0 collective-permute-done.3.refs_8_.behind_ref.behind1_ref
  22.1 0.0 collective-permute-start.4
  22.2 0.6 shard_map.60
  22.7 3.1 %collective-permute-start.8 = (bf16[2,128,384]{2,1,0:T(8,128)(2,1)S(1)}, bf16[2,128,384]{2,1,0:T(8,128)(2,1)S(1)}, u32[]{:S(2)}, u32[]{:S(2)}) collective-permute-start(bf16[2,128,384]{2,1,0:T(8,128)(2,1)S(1)} %shard_map.60), channel_id=1, source_target_pairs={{0,96},{128,224},{1,97},{129,225},{2,98},{130,226},{3,99},{131,227... | collective-permute-start | bytes 589832 | tf_op jit(solution)/shard_map/ppermute | solution.py:30
  25.8 0.6 shard_map.61
  26.4 0.1 collective-permute-start.10
  26.5 4.1 %collective-permute-start.9 = (bf16[128,384]{1,0:T(8,128)(2,1)S(1)}, bf16[128,384]{1,0:T(8,128)(2,1)S(1)}, u32[]{:S(2)}, u32[]{:S(2)}) collective-permute-start(bf16[128,384]{1,0:T(8,128)(2,1)S(1)} %get-tuple-element.9), channel_id=1, source_target_pairs={{0,99},{128,3},{1,96},{129,0},{2,97},{130,1},{3,98},{131,2},{16,11... | collective-permute-start | bytes 294920 | tf_op jit(solution)/shard_map/ppermute | solution.py:30
  30.6 1.7 %collective-permute-done.10.second_ref = bf16[128,384]{1,0:T(8,128)(2,1)S(1)} collective-permute-done((bf16[128,384]{1,0:T(8,128)(2,1)S(1)}, bf16[128,384]{1,0:T(8,128)(2,1)S(1)}, u32[]{:S(2)}, u32[]{:S(2)}) %collective-permute-start.10) | collective-permute-done | bytes 98336 | tf_op jit(solution)/shard_map/ppermute | solution.py:30
  32.3 1.5 %collective-permute-done.9.first_ref = bf16[128,384]{1,0:T(8,128)(2,1)S(1)} collective-permute-done((bf16[128,384]{1,0:T(8,128)(2,1)S(1)}, bf16[128,384]{1,0:T(8,128)(2,1)S(1)}, u32[]{:S(2)}, u32[]{:S(2)}) %collective-permute-start.9) | collective-permute-done | bytes 98336 | tf_op jit(solution)/shard_map/ppermute | solution.py:30
  33.8 3.5 %collective-permute-done.4.refs_7_.behind2_ref = bf16[128,1536]{1,0:T(8,128)(2,1)S(1)} collective-permute-done((bf16[128,1536]{1,0:T(8,128)(2,1)S(1)}, bf16[128,1536]{1,0:T(8,128)(2,1)S(1)}, u32[]{:S(2)}, u32[]{:S(2)}) %collective-permute-start.4) | collective-permute-done | bytes 393248 | tf_op jit(solution)/shard_map/ppermute | solution.py:30
  37.3 0.6 shard_map.62.refs_0_
  37.9 1.7 %collective-permute-start.11 = (bf16[4,128,384]{2,1,0:T(8,128)(2,1)S(1)}, bf16[4,128,384]{2,1,0:T(8,128)(2,1)S(1)}, u32[]{:S(2)}, u32[]{:S(2)}) collective-permute-start(bf16[4,128,384]{2,1,0:T(8,128)(2,1)S(1)} %shard_map.62.refs_0_), channel_id=1, source_target_pairs={{0,32},{128,160},{1,33},{129,161},{2,34},{130,162},{3,35},{131,163... | collective-permute-start | bytes 1179656 | tf_op jit(solution)/shard_map/ppermute | solution.py:30
  39.6 1.7 %collective-permute-start.13 = (bf16[4,128,384]{2,1,0:T(8,128)(2,1)S(1)}, bf16[4,128,384]{2,1,0:T(8,128)(2,1)S(1)}, u32[]{:S(2)}, u32[]{:S(2)}) collective-permute-start(bf16[4,128,384]{2,1,0:T(8,128)(2,1)S(1)} %shard_map.62.refs_0_), channel_id=1, source_target_pairs={{0,96},{128,224},{1,97},{129,225},{2,98},{130,226},{3,99},{131,227... | collective-permute-start | bytes 1179656 | tf_op jit(solution)/shard_map/ppermute | solution.py:30
  41.2 5.9 %collective-permute-done.11.refs_1_ = bf16[4,128,384]{2,1,0:T(8,128)(2,1)S(1)} collective-permute-done((bf16[4,128,384]{2,1,0:T(8,128)(2,1)S(1)}, bf16[4,128,384]{2,1,0:T(8,128)(2,1)S(1)}, u32[]{:S(2)}, u32[]{:S(2)}) %collective-permute-start.11) | collective-permute-done | bytes 393248 | tf_op jit(solution)/shard_map/ppermute | solution.py:30
  47.1 0.2 collective-permute-done.13.refs_2_
  47.3 0.1 shard_map.64.refs_0_
  47.4 0.1 collective-permute-start.16
  47.5 3.3 %collective-permute-start.5 = (bf16[128,1536]{1,0:T(8,128)(2,1)S(1)}, bf16[128,1536]{1,0:T(8,128)(2,1)S(1)}, u32[]{:S(2)}, u32[]{:S(2)}) collective-permute-start(bf16[128,1536]{1,0:T(8,128)(2,1)S(1)} %collective-permute-done.4.refs_7_.behind2_ref), channel_id=1, source_target_pairs={{0,128},{128,1},{1,129},{129,2},{2,130},{130,3},{3,131},{131,0},{1... | collective-permute-start | bytes 1179656 | tf_op jit(solution)/shard_map/ppermute | solution.py:30
  50.9 0.0 collective-permute-start.2
  50.9 0.3 collective-permute-start.12
  51.2 3.1 %collective-permute-start.14 = (bf16[2,128,384]{2,1,0:T(8,128)(2,1)S(1)}, bf16[2,128,384]{2,1,0:T(8,128)(2,1)S(1)}, u32[]{:S(2)}, u32[]{:S(2)}) collective-permute-start(bf16[2,128,384]{2,1,0:T(8,128)(2,1)S(1)} %slice.35), channel_id=1, source_target_pairs={{0,96},{128,224},{1,97},{129,225},{2,98},{130,226},{3,99},{131,227... | collective-permute-start | bytes 589832 | tf_op jit(solution)/shard_map/ppermute | solution.py:30
  54.3 4.8 %collective-permute-done.12.refs_0_ = bf16[2,128,384]{2,1,0:T(8,128)(2,1)S(1)} collective-permute-done((bf16[2,128,384]{2,1,0:T(8,128)(2,1)S(1)}, bf16[2,128,384]{2,1,0:T(8,128)(2,1)S(1)}, u32[]{:S(2)}, u32[]{:S(2)}) %collective-permute-start.12) | collective-permute-done | bytes 196640 | tf_op jit(solution)/shard_map/ppermute | solution.py:30
  59.1 0.0 collective-permute-done.14.refs_1_
  59.2 0.1 collective-permute-start.15
  59.3 1.0 collective-permute-done.5.refs_6_
  60.3 2.3 %collective-permute-start.6 = (bf16[64,1536]{1,0:T(8,128)(2,1)S(1)}, bf16[64,1536]{1,0:T(8,128)(2,1)S(1)}, u32[]{:S(2)}, u32[]{:S(2)}) collective-permute-start(bf16[64,1536]{1,0:T(8,128)(2,1)S(1)} %slice.32), channel_id=1, source_target_pairs={{0,128},{128,1},{1,129},{129,2},{2,130},{130,3},{3,131},{131,0},{1... | collective-permute-start | bytes 589832 | tf_op jit(solution)/shard_map/ppermute | solution.py:30
  62.6 1.3 collective-permute-start.7
  63.9 4.2 %collective-permute-done.6.refs_4_ = bf16[64,1536]{1,0:T(8,128)(2,1)S(1)} collective-permute-done((bf16[64,1536]{1,0:T(8,128)(2,1)S(1)}, bf16[64,1536]{1,0:T(8,128)(2,1)S(1)}, u32[]{:S(2)}, u32[]{:S(2)}) %collective-permute-start.6) | collective-permute-done | bytes 196640 | tf_op jit(solution)/shard_map/ppermute | solution.py:30
  68.1 0.6 collective-permute-done.7.refs_5_
  68.8 0.2 shard_map.59
  69.0 0.0 collective-permute-done.16.refs_2_
  69.0 0.9 shard_map.65.refs_1_
  69.9 0.6 shard_map.66
  70.5 1.8 %convolution_convert_fusion = bf16[1536,384]{1,0:T(8,128)(2,1)S(1)} fusion(bf16[1024,1536]{1,0:T(8,128)(2,1)S(1)} %shard_map.59, bf16[4,1024,384]{2,1,0:T(8,128)(2,1)S(1)} %shard_map.66), kind=kOutput, calls=%fused_computation | convolution fusion | flops 1208549376 | bytes 5111808 | tf_op jit(solution)/shard_map/dot_general | solution.py:205
  72.3 0.9 collective-permute-start.18
  73.2 2.9 %convolution_convert_fusion.1 = bf16[1536,384]{1,0:T(8,128)(2,1)} fusion(bf16[1024,1536]{1,0:T(8,128)(2,1)S(1)} %shard_map.59, bf16[4,1024,384]{2,1,0:T(8,128)(2,1)S(1)} %shard_map.66), kind=kOutput, calls=%fused_computation.1 | convolution fusion | flops 1208549376 | bytes 5111808 | tf_op jit(solution)/shard_map/dot_general | solution.py:205
  76.1 1.2 collective-permute-start.17
  77.3 1.8 %fusion = f32[1536,384]{1,0:T(8,128)S(1)} fusion(bf16[1024,1536]{1,0:T(8,128)(2,1)S(1)} %shard_map.59, bf16[4,1024,384]{2,1,0:T(8,128)(2,1)S(1)} %shard_map.66), kind=kOutput, calls=%fused_computation.8 | convolution fusion | flops 1207959552 | bytes 6291456 | tf_op jit(solution)/shard_map/dot_general | solution.py:205
  79.2 1.8 %fusion.1 = f32[1536,384]{1,0:T(8,128)S(1)} fusion(bf16[1024,1536]{1,0:T(8,128)(2,1)S(1)} %shard_map.59, bf16[4,1024,384]{2,1,0:T(8,128)(2,1)S(1)} %shard_map.66), kind=kOutput, calls=%fused_computation.10 | convolution fusion | flops 1207959552 | bytes 6291456 | tf_op jit(solution)/shard_map/dot_general | solution.py:205
  81.0 7.6 %collective-permute-done.18 = bf16[1536,384]{1,0:T(8,128)(2,1)S(1)} collective-permute-done((bf16[1536,384]{1,0:T(8,128)(2,1)S(1)}, bf16[1536,384]{1,0:T(8,128)(2,1)S(1)}, u32[]{:S(2)}, u32[]{:S(2)}) %collective-permute-start.18) | collective-permute-done | bytes 1179680 | tf_op jit(solution)/shard_map/ppermute | solution.py:30
  88.6 1.3 add_convert_fusion
  89.9 0.5 collective-permute-start.19
  90.4 1.0 collective-permute-start.20
  91.4 20.1 %collective-permute-done.20 = f32[1536]{0:T(1024)S(1)} collective-permute-done((f32[1536]{0:T(1024)S(1)}, f32[1536]{0:T(1024)S(1)}, u32[]{:S(2)}, u32[]{:S(2)}) %collective-permute-start.20) | collective-permute-done | bytes 6176 | tf_op jit(solution)/shard_map/ppermute | solution.py:30
  111.5 0.5 collective-permute-start.21
  111.9 4.4 %collective-permute-done.21 = f32[1536]{0:T(1024)S(1)} collective-permute-done((f32[1536]{0:T(1024)S(1)}, f32[1536]{0:T(1024)S(1)}, u32[]{:S(2)}, u32[]{:S(2)}) %collective-permute-start.21) | collective-permute-done | bytes 6176 | tf_op jit(solution)/shard_map/ppermute | solution.py:30
  116.3 1.5 %collective-permute-start.22 = (f32[1536]{0:T(1024)S(1)}, f32[1536]{0:T(1024)S(1)}, u32[]{:S(2)}, u32[]{:S(2)}) collective-permute-start(f32[1536]{0:T(1024)S(1)} %add.53), channel_id=1, source_target_pairs={{0,128},{128,0},{1,129},{129,1},{2,130},{130,2},{3,131},{131,3},{1... | collective-permute-start | bytes 18440 | tf_op jit(solution)/shard_map/ppermute | solution.py:30
  117.8 2.2 %collective-permute-done.22 = f32[1536]{0:T(1024)S(1)} collective-permute-done((f32[1536]{0:T(1024)S(1)}, f32[1536]{0:T(1024)S(1)}, u32[]{:S(2)}, u32[]{:S(2)}) %collective-permute-start.22) | collective-permute-done | bytes 6176 | tf_op jit(solution)/shard_map/ppermute | solution.py:30
  120.0 1.2 collective-permute-start.23
  121.2 3.4 %collective-permute-done.23 = f32[1536]{0:T(1024)S(1)} collective-permute-done((f32[1536]{0:T(1024)S(1)}, f32[1536]{0:T(1024)S(1)}, u32[]{:S(2)}, u32[]{:S(2)}) %collective-permute-start.23) | collective-permute-done | bytes 6176 | tf_op jit(solution)/shard_map/ppermute | solution.py:30
  124.6 1.4 %collective-permute-start.24 = (f32[1536]{0:T(1024)S(1)}, f32[1536]{0:T(1024)S(1)}, u32[]{:S(2)}, u32[]{:S(2)}) collective-permute-start(f32[1536]{0:T(1024)S(1)} %add.55), channel_id=1, source_target_pairs={{0,2},{128,130},{1,3},{129,131},{2,0},{130,128},{3,1},{131,129},{1... | collective-permute-start | bytes 18440 | tf_op jit(solution)/shard_map/ppermute | solution.py:30
  126.0 6.1 %collective-permute-done.24 = f32[1536]{0:T(1024)S(1)} collective-permute-done((f32[1536]{0:T(1024)S(1)}, f32[1536]{0:T(1024)S(1)}, u32[]{:S(2)}, u32[]{:S(2)}) %collective-permute-start.24) | collective-permute-done | bytes 6176 | tf_op jit(solution)/shard_map/ppermute | solution.py:30
  132.1 0.6 add_multiply_fusion.1
  132.7 0.0 collective-permute-done.17
  132.7 0.2 convert_add_fusion
  132.9 3.0 %add_multiply_fusion = f32[1536,384]{1,0:T(8,128)} fusion(f32[1536,384]{1,0:T(8,128)S(1)} %convert_add_fusion, bf16[1536,384]{1,0:T(8,128)(2,1)} %collective-permute-done.19), kind=kLoop, calls=%fused_computation.2 | loop fusion | flops 1769472 | bytes 5898240 | tf_op jit(solution)/shard_map/mul | solution.py:280
  (17 shorter events, 0.2 us)
Async XLA Ops:
  2.2 1.0 copy-start
  4.1 14.3 %collective-permute-start = (bf16[128,1536]{1,0:T(8,128)(2,1)S(1)}, bf16[128,1536]{1,0:T(8,128)(2,1)S(1)}, u32[]{:S(2)}, u32[]{:S(2)}) collective-permute-start(bf16[128,1536]{1,0:T(8,128)(2,1)S(1)} %get-tuple-element.8.refs_0_.first_ref), channel_id=1, source_target_pairs={{0,131},{128,0},{1,128},{129,1},{2,129},{130,2},{3,130},{131,3},{1... | collective-permute-start | bytes 1179656 | tf_op jit(solution)/shard_map/ppermute | solution.py:30
  10.1 12.1 %collective-permute-start.3 = (bf16[128,1536]{1,0:T(8,128)(2,1)S(1)}, bf16[128,1536]{1,0:T(8,128)(2,1)S(1)}, u32[]{:S(2)}, u32[]{:S(2)}) collective-permute-start(bf16[128,1536]{1,0:T(8,128)(2,1)S(1)} %get-tuple-element.8.refs_0_.first_ref), channel_id=1, source_target_pairs={{0,128},{128,1},{1,129},{129,2},{2,130},{130,3},{3,131},{131,0},{1... | collective-permute-start | bytes 1179656 | tf_op jit(solution)/shard_map/ppermute | solution.py:30
  18.5 15.4 %collective-permute-start.1 = (bf16[128,1536]{1,0:T(8,128)(2,1)S(1)}, bf16[128,1536]{1,0:T(8,128)(2,1)S(1)}, u32[]{:S(2)}, u32[]{:S(2)}) collective-permute-start(bf16[128,1536]{1,0:T(8,128)(2,1)S(1)} %collective-permute-done.refs_1_.second_ref.ahead_ref), channel_id=1, source_target_pairs={{0,131},{128,0},{1,128},{129,1},{2,129},{130,2},{3,130},{131,3},{1... | collective-permute-start | bytes 1179656 | tf_op jit(solution)/shard_map/ppermute | solution.py:30
  22.1 15.1 %collective-permute-start.4 = (bf16[128,1536]{1,0:T(8,128)(2,1)S(1)}, bf16[128,1536]{1,0:T(8,128)(2,1)S(1)}, u32[]{:S(2)}, u32[]{:S(2)}) collective-permute-start(bf16[128,1536]{1,0:T(8,128)(2,1)S(1)} %collective-permute-done.3.refs_8_.behind_ref.behind1_ref), channel_id=1, source_target_pairs={{0,128},{128,1},{1,129},{129,2},{2,130},{130,3},{3,131},{131,0},{1... | collective-permute-start | bytes 1179656 | tf_op jit(solution)/shard_map/ppermute | solution.py:30
  22.7 11.1 %collective-permute-start.8 = (bf16[2,128,384]{2,1,0:T(8,128)(2,1)S(1)}, bf16[2,128,384]{2,1,0:T(8,128)(2,1)S(1)}, u32[]{:S(2)}, u32[]{:S(2)}) collective-permute-start(bf16[2,128,384]{2,1,0:T(8,128)(2,1)S(1)} %shard_map.60), channel_id=1, source_target_pairs={{0,96},{128,224},{1,97},{129,225},{2,98},{130,226},{3,99},{131,227... | collective-permute-start | bytes 589832 | tf_op jit(solution)/shard_map/ppermute | solution.py:30
  26.4 5.9 %collective-permute-start.10 = (bf16[128,384]{1,0:T(8,128)(2,1)S(1)}, bf16[128,384]{1,0:T(8,128)(2,1)S(1)}, u32[]{:S(2)}, u32[]{:S(2)}) collective-permute-start(bf16[128,384]{1,0:T(8,128)(2,1)S(1)} %get-tuple-element.10), channel_id=1, source_target_pairs={{0,97},{128,224},{1,98},{129,225},{2,99},{130,226},{3,96},{131,227... | collective-permute-start | bytes 294920 | tf_op jit(solution)/shard_map/ppermute | solution.py:30
  26.5 7.3 %collective-permute-start.9 = (bf16[128,384]{1,0:T(8,128)(2,1)S(1)}, bf16[128,384]{1,0:T(8,128)(2,1)S(1)}, u32[]{:S(2)}, u32[]{:S(2)}) collective-permute-start(bf16[128,384]{1,0:T(8,128)(2,1)S(1)} %get-tuple-element.9), channel_id=1, source_target_pairs={{0,99},{128,3},{1,96},{129,0},{2,97},{130,1},{3,98},{131,2},{16,11... | collective-permute-start | bytes 294920 | tf_op jit(solution)/shard_map/ppermute | solution.py:30
  37.9 9.2 %collective-permute-start.11 = (bf16[4,128,384]{2,1,0:T(8,128)(2,1)S(1)}, bf16[4,128,384]{2,1,0:T(8,128)(2,1)S(1)}, u32[]{:S(2)}, u32[]{:S(2)}) collective-permute-start(bf16[4,128,384]{2,1,0:T(8,128)(2,1)S(1)} %shard_map.62.refs_0_), channel_id=1, source_target_pairs={{0,32},{128,160},{1,33},{129,161},{2,34},{130,162},{3,35},{131,163... | collective-permute-start | bytes 1179656 | tf_op jit(solution)/shard_map/ppermute | solution.py:30
  39.6 7.8 %collective-permute-start.13 = (bf16[4,128,384]{2,1,0:T(8,128)(2,1)S(1)}, bf16[4,128,384]{2,1,0:T(8,128)(2,1)S(1)}, u32[]{:S(2)}, u32[]{:S(2)}) collective-permute-start(bf16[4,128,384]{2,1,0:T(8,128)(2,1)S(1)} %shard_map.62.refs_0_), channel_id=1, source_target_pairs={{0,96},{128,224},{1,97},{129,225},{2,98},{130,226},{3,99},{131,227... | collective-permute-start | bytes 1179656 | tf_op jit(solution)/shard_map/ppermute | solution.py:30
  47.4 21.5 %collective-permute-start.16 = (bf16[12,128,384]{2,1,0:T(8,128)(2,1)S(1)}, bf16[12,128,384]{2,1,0:T(8,128)(2,1)S(1)}, u32[]{:S(2)}, u32[]{:S(2)}) collective-permute-start(bf16[12,128,384]{2,1,0:T(8,128)(2,1)S(1)} %shard_map.64.refs_0_), channel_id=1, source_target_pairs={{0,16},{128,144},{1,17},{129,145},{2,18},{130,146},{3,19},{131,147... | collective-permute-start | bytes 3538952 | tf_op jit(solution)/shard_map/ppermute | solution.py:30
  47.5 12.7 %collective-permute-start.5 = (bf16[128,1536]{1,0:T(8,128)(2,1)S(1)}, bf16[128,1536]{1,0:T(8,128)(2,1)S(1)}, u32[]{:S(2)}, u32[]{:S(2)}) collective-permute-start(bf16[128,1536]{1,0:T(8,128)(2,1)S(1)} %collective-permute-done.4.refs_7_.behind2_ref), channel_id=1, source_target_pairs={{0,128},{128,1},{1,129},{129,2},{2,130},{130,3},{3,131},{131,0},{1... | collective-permute-start | bytes 1179656 | tf_op jit(solution)/shard_map/ppermute | solution.py:30
  50.9 11.7 %collective-permute-start.2 = (bf16[128,1536]{1,0:T(8,128)(2,1)S(1)}, bf16[128,1536]{1,0:T(8,128)(2,1)S(1)}, u32[]{:S(2)}, u32[]{:S(2)}) collective-permute-start(bf16[128,1536]{1,0:T(8,128)(2,1)S(1)} %collective-permute-done.1.refs_2_.ahead2_ref), channel_id=1, source_target_pairs={{0,131},{128,0},{1,128},{129,1},{2,129},{130,2},{3,130},{131,3},{1... | collective-permute-start | bytes 1179656 | tf_op jit(solution)/shard_map/ppermute | solution.py:30
  50.9 8.2 %collective-permute-start.12 = (bf16[2,128,384]{2,1,0:T(8,128)(2,1)S(1)}, bf16[2,128,384]{2,1,0:T(8,128)(2,1)S(1)}, u32[]{:S(2)}, u32[]{:S(2)}) collective-permute-start(bf16[2,128,384]{2,1,0:T(8,128)(2,1)S(1)} %slice.34), channel_id=1, source_target_pairs={{0,32},{128,160},{1,33},{129,161},{2,34},{130,162},{3,35},{131,163... | collective-permute-start | bytes 589832 | tf_op jit(solution)/shard_map/ppermute | solution.py:30
  51.2 8.0 %collective-permute-start.14 = (bf16[2,128,384]{2,1,0:T(8,128)(2,1)S(1)}, bf16[2,128,384]{2,1,0:T(8,128)(2,1)S(1)}, u32[]{:S(2)}, u32[]{:S(2)}) collective-permute-start(bf16[2,128,384]{2,1,0:T(8,128)(2,1)S(1)} %slice.35), channel_id=1, source_target_pairs={{0,96},{128,224},{1,97},{129,225},{2,98},{130,226},{3,99},{131,227... | collective-permute-start | bytes 589832 | tf_op jit(solution)/shard_map/ppermute | solution.py:30
  59.2 10.7 %collective-permute-start.15 = (bf16[4,128,384]{2,1,0:T(8,128)(2,1)S(1)}, bf16[4,128,384]{2,1,0:T(8,128)(2,1)S(1)}, u32[]{:S(2)}, u32[]{:S(2)}) collective-permute-start(bf16[4,128,384]{2,1,0:T(8,128)(2,1)S(1)} %shard_map.63.refs_1_), channel_id=1, source_target_pairs={{0,16},{128,144},{1,17},{129,145},{2,18},{130,146},{3,19},{131,147... | collective-permute-start | bytes 1179656 | tf_op jit(solution)/shard_map/ppermute | solution.py:30
  60.3 7.8 %collective-permute-start.6 = (bf16[64,1536]{1,0:T(8,128)(2,1)S(1)}, bf16[64,1536]{1,0:T(8,128)(2,1)S(1)}, u32[]{:S(2)}, u32[]{:S(2)}) collective-permute-start(bf16[64,1536]{1,0:T(8,128)(2,1)S(1)} %slice.32), channel_id=1, source_target_pairs={{0,128},{128,1},{1,129},{129,2},{2,130},{130,3},{3,131},{131,0},{1... | collective-permute-start | bytes 589832 | tf_op jit(solution)/shard_map/ppermute | solution.py:30
  62.6 6.2 %collective-permute-start.7 = (bf16[64,1536]{1,0:T(8,128)(2,1)S(1)}, bf16[64,1536]{1,0:T(8,128)(2,1)S(1)}, u32[]{:S(2)}, u32[]{:S(2)}) collective-permute-start(bf16[64,1536]{1,0:T(8,128)(2,1)S(1)} %slice.33), channel_id=1, source_target_pairs={{0,131},{128,0},{1,128},{129,1},{2,129},{130,2},{3,130},{131,3},{1... | collective-permute-start | bytes 589832 | tf_op jit(solution)/shard_map/ppermute | solution.py:30
  72.3 16.3 %collective-permute-start.18 = (bf16[1536,384]{1,0:T(8,128)(2,1)S(1)}, bf16[1536,384]{1,0:T(8,128)(2,1)S(1)}, u32[]{:S(2)}, u32[]{:S(2)}) collective-permute-start(bf16[1536,384]{1,0:T(8,128)(2,1)S(1)} %convolution_convert_fusion), channel_id=1, source_target_pairs={{0,4},{128,132},{1,5},{129,133},{2,6},{130,134},{3,7},{131,135},{1... | collective-permute-start | bytes 3538952 | tf_op jit(solution)/shard_map/ppermute | solution.py:30
  76.1 56.6 %collective-permute-start.17 = (bf16[1536,384]{1,0:T(8,128)(2,1)}, bf16[1536,384]{1,0:T(8,128)(2,1)S(1)}, u32[]{:S(2)}, u32[]{:S(2)}) collective-permute-start(bf16[1536,384]{1,0:T(8,128)(2,1)} %convolution_convert_fusion.1), channel_id=1, source_target_pairs={{0,4},{128,132},{1,5},{129,133},{2,6},{130,134},{3,7},{131,135},{1... | collective-permute-start | bytes 3538952 | tf_op jit(solution)/shard_map/ppermute | solution.py:30
  89.9 43.0 %collective-permute-start.19 = (bf16[1536,384]{1,0:T(8,128)(2,1)}, bf16[1536,384]{1,0:T(8,128)(2,1)}, u32[]{:S(2)}, u32[]{:S(2)}) collective-permute-start(bf16[1536,384]{1,0:T(8,128)(2,1)} %add_convert_fusion), channel_id=1, source_target_pairs={{0,12},{128,140},{1,13},{129,141},{2,14},{130,142},{3,15},{131,143... | collective-permute-start | bytes 3538952 | tf_op jit(solution)/shard_map/ppermute | solution.py:30
  90.4 21.0 %collective-permute-start.20 = (f32[1536]{0:T(1024)S(1)}, f32[1536]{0:T(1024)S(1)}, u32[]{:S(2)}, u32[]{:S(2)}) collective-permute-start(f32[1536]{0:T(1024)S(1)} %reduce), channel_id=1, source_target_pairs={{0,4},{128,132},{1,5},{129,133},{2,6},{130,134},{3,7},{131,135},{1... | collective-permute-start | bytes 18440 | tf_op jit(solution)/shard_map/ppermute | solution.py:30
  111.5 4.9 %collective-permute-start.21 = (f32[1536]{0:T(1024)S(1)}, f32[1536]{0:T(1024)S(1)}, u32[]{:S(2)}, u32[]{:S(2)}) collective-permute-start(f32[1536]{0:T(1024)S(1)} %add.52), channel_id=1, source_target_pairs={{0,12},{128,140},{1,13},{129,141},{2,14},{130,142},{3,15},{131,143... | collective-permute-start | bytes 18440 | tf_op jit(solution)/shard_map/ppermute | solution.py:30
  116.3 3.7 %collective-permute-start.22 = (f32[1536]{0:T(1024)S(1)}, f32[1536]{0:T(1024)S(1)}, u32[]{:S(2)}, u32[]{:S(2)}) collective-permute-start(f32[1536]{0:T(1024)S(1)} %add.53), channel_id=1, source_target_pairs={{0,128},{128,0},{1,129},{129,1},{2,130},{130,2},{3,131},{131,3},{1... | collective-permute-start | bytes 18440 | tf_op jit(solution)/shard_map/ppermute | solution.py:30
  120.0 4.5 %collective-permute-start.23 = (f32[1536]{0:T(1024)S(1)}, f32[1536]{0:T(1024)S(1)}, u32[]{:S(2)}, u32[]{:S(2)}) collective-permute-start(f32[1536]{0:T(1024)S(1)} %add.54), channel_id=1, source_target_pairs={{0,1},{128,129},{1,0},{129,128},{2,3},{130,131},{3,2},{131,130},{1... | collective-permute-start | bytes 18440 | tf_op jit(solution)/shard_map/ppermute | solution.py:30
  124.6 7.6 %collective-permute-start.24 = (f32[1536]{0:T(1024)S(1)}, f32[1536]{0:T(1024)S(1)}, u32[]{:S(2)}, u32[]{:S(2)}) collective-permute-start(f32[1536]{0:T(1024)S(1)} %add.55), channel_id=1, source_target_pairs={{0,2},{128,130},{1,3},{129,131},{2,0},{130,128},{3,1},{131,129},{1... | collective-permute-start | bytes 18440 | tf_op jit(solution)/shard_map/ppermute | solution.py:30
